TPU v7x, 32 devices: a whole 2x2x4 slice. The times are simulated.
32 devices in a mesh: patch: 8 (over z, y), hidden: 4 (over x, core).
Axes of the slice: x: 2, y: 2, z: 4, core: 2. Of those that a mesh axis runs over, the one named last changes fastest.
Arguments:
- grid_latent: bfloat16 [24576, 512], P('patch'), may hold values from -6 to 6
- mesh_latent: bfloat16 [40960, 512], P('patch'), may hold values from -6 to 6
- edge_latent: bfloat16 [65536, 512], P('patch'), may hold values from -6 to 6
- senders: int32 [65536], P('patch'), may hold values from 0 to 24575, as said below
- receivers: int32 [65536], P('patch'), may hold values from 0 to 40959
- mesh_slot: int32 [40960], replicated, may hold values from 0 to 40959, as said below
- edge_counts: int32 [8], P('patch'), may hold values from 2730 to 8192, as said below
- w_edge: bfloat16 [512, 512], P(None, 'hidden'), may hold values from -0.25 to 0.25
- w_sender: bfloat16 [512, 512], P(None, 'hidden'), may hold values from -0.25 to 0.25
- w_receiver: bfloat16 [512, 512], P(None, 'hidden'), may hold values from -0.25 to 0.25
- edge_bias: float32 [512], P('hidden'), may hold values from -3 to 3
- w_edge_out: bfloat16 [512, 512], P('hidden'), may hold values from -0.25 to 0.25
- edge_out_bias: float32 [512], P('hidden'), may hold values from -3 to 3
- edge_gain: float32 [512], P('hidden'), may hold values from 0.25 to 1.75
- edge_shift: float32 [512], P('hidden'), may hold values from -2 to 2
- w_mesh_in: bfloat16 [512, 512], P(None, 'hidden'), may hold values from -0.25 to 0.25
- w_message_in: bfloat16 [512, 512], P(None, 'hidden'), may hold values from -0.25 to 0.25
- mesh_bias: float32 [512], P('hidden'), may hold values from -3 to 3
- w_mesh_out: bfloat16 [512, 512], P('hidden'), may hold values from -0.25 to 0.25
- mesh_out_bias: float32 [512], P('hidden'), may hold values from -3 to 3
- mesh_gain: float32 [512], P('hidden'), may hold values from 0.25 to 1.75
- mesh_shift: float32 [512], P('hidden'), may hold values from -2 to 2
Outputs:
- mesh_out: bfloat16 [40960, 512], P('patch', 'hidden')
- edge_out: bfloat16 [65536, 512], P('patch', 'hidden')
Inputs may be any that keep to these rules, and one draw needn't show every extreme that they name: `mesh_slot`: A permutation of the mesh node ids 0 to 40959; owner block p holds mesh rows p * 5120 to (p + 1) * 5120 - 1. `senders`: edge slots of block p (slots p * 8192 to (p + 1) * 8192 - 1) send from grid nodes p * 3072 to (p + 1) * 3072 - 1. Only the first edge_counts[p] slots of block p are live; some block is full.
All inputs are finite; a program needn't handle non-finite values.
Results may differ from a plain program's by a relative error of at most 0.014.
Values may be sent and summed in bfloat16 or wider, within the bound.
A program may use at most 192 MiB of HBM per device.

v0:
```python
import functools

import jax
import jax.numpy as jnp
from jax import lax
from jax.experimental import pallas as pl
from jax.experimental.pallas import tpu as pltpu
from jax.sharding import PartitionSpec as P

EPSILON = 1e-05
CHUNKS = 2


def row_block(rows, most):
    block = most
    while rows % block:
        block //= 2
    return block


def norm_own(total, gain, offset):
    width = total.shape[1]
    own = gain.shape[1]
    center = jnp.sum(total, axis=1, keepdims=True) / width
    centered = total - center
    spread = jnp.sum(centered * centered, axis=1, keepdims=True) / width
    return centered[:, :own] * lax.rsqrt(spread + EPSILON) * gain + offset


def own_columns(column, latent, own, block, first):
    if own % 128 == 0:
        return latent, pl.BlockSpec((block, own), lambda i, c: (i + first, c[0]))
    cut = lax.dynamic_slice_in_dim(latent, column[0] * own, own, 1)
    return cut, pl.BlockSpec((block, own), lambda i, c: (i + first, 0))


def edge_kernel(first_row, scalars, hidden_ref, latent_ref, w_ref, bias_ref, gain_ref, shift_ref, message_ref, out_ref):
    total = jnp.dot(hidden_ref[...], w_ref[...], preferred_element_type=jnp.float32) + bias_ref[...]
    start = first_row + pl.program_id(0) * total.shape[0]
    slot = start + lax.broadcasted_iota(jnp.int32, message_ref.shape, 0)
    message = norm_own(total, gain_ref[...], shift_ref[...])
    message = jnp.where(slot < scalars[1], message, 0.0)
    message_ref[...] = message
    out_ref[...] = (latent_ref[...].astype(jnp.float32) + message).astype(out_ref.dtype)


def edge_finish(column, hidden, latent, first_row, w_out, bias, gain, shift):
    rows, full = hidden.shape
    own = gain.shape[1]
    block = row_block(rows, 1024)
    first = first_row // block
    latent, latent_spec = own_columns(column, latent, own, block, first)
    return pl.pallas_call(
        functools.partial(edge_kernel, first_row),
        grid_spec=pltpu.PrefetchScalarGridSpec(
            num_scalar_prefetch=1,
            grid=(rows // block,),
            in_specs=[
                pl.BlockSpec((block, full), lambda i, c: (i, 0)),
                latent_spec,
                pl.BlockSpec((full, full), lambda i, c: (0, 0)),
                pl.BlockSpec((1, full), lambda i, c: (0, 0)),
                pl.BlockSpec((1, own), lambda i, c: (0, 0)),
                pl.BlockSpec((1, own), lambda i, c: (0, 0)),
            ],
            out_specs=[
                pl.BlockSpec((block, own), lambda i, c: (i, 0)),
                pl.BlockSpec((block, own), lambda i, c: (i, 0)),
            ],
        ),
        out_shape=[
            jax.ShapeDtypeStruct((rows, own), jnp.float32),
            jax.ShapeDtypeStruct((rows, own), jnp.bfloat16),
        ],
        cost_estimate=pl.CostEstimate(
            flops=2 * rows * full * full, bytes_accessed=2 * rows * full + 8 * rows * own, transcendentals=0
        ),
        name="edge_finish",
    )(column, hidden, latent, w_out, bias, gain, shift)


def mesh_kernel(column, latent_ref, own_ref, summed_ref, w_in_ref, w_msg_ref, bias_in_ref, w_out_ref, bias_ref, gain_ref, shift_ref, out_ref):
    pre = jnp.dot(latent_ref[...], w_in_ref[...], preferred_element_type=jnp.float32)
    summed = jnp.concatenate([summed_ref[h] for h in range(summed_ref.shape[0])], axis=1)
    pre = pre + jnp.dot(summed, w_msg_ref[...], preferred_element_type=jnp.float32) + bias_in_ref[...]
    hidden = jax.nn.silu(pre).astype(jnp.bfloat16)
    total = jnp.dot(hidden, w_out_ref[...], preferred_element_type=jnp.float32) + bias_ref[...]
    update = norm_own(total, gain_ref[...], shift_ref[...])
    out_ref[...] = (own_ref[...].astype(jnp.float32) + update).astype(out_ref.dtype)


def mesh_finish(column, latent, summed, w_in, w_msg, bias_in, w_out, bias, gain, shift):
    rows, full = latent.shape
    own = gain.shape[1]
    block = row_block(rows, 1024)
    whole = lambda i, c: (0, 0)
    own_latent, own_spec = own_columns(column, latent, own, block, 0)
    return pl.pallas_call(
        mesh_kernel,
        grid_spec=pltpu.PrefetchScalarGridSpec(
            num_scalar_prefetch=1,
            grid=(rows // block,),
            in_specs=[
                pl.BlockSpec((block, full), lambda i, c: (i, 0)),
                own_spec,
                pl.BlockSpec((summed.shape[0], block, summed.shape[2]), lambda i, c: (0, i, 0)),
                pl.BlockSpec((full, full), whole),
                pl.BlockSpec((full, full), whole),
                pl.BlockSpec((1, full), whole),
                pl.BlockSpec((full, full), whole),
                pl.BlockSpec((1, full), whole),
                pl.BlockSpec((1, own), whole),
                pl.BlockSpec((1, own), whole),
            ],
            out_specs=pl.BlockSpec((block, own), lambda i, c: (i, 0)),
        ),
        out_shape=jax.ShapeDtypeStruct((rows, own), jnp.bfloat16),
        cost_estimate=pl.CostEstimate(
            flops=6 * rows * full * full, bytes_accessed=4 * rows * full + 4 * rows * own, transcendentals=rows * full
        ),
        name="mesh_finish",
    )(column, latent, own_latent, summed, w_in, w_msg, bias_in, w_out, bias, gain, shift)


def combine_kernel(sizes, part_ref, out_ref, stage, leaving, own, paired, crossed, gathered, own_sem, pair_send, pair_recv, cross_send, cross_recv, side_send, side_recv, far_send, far_recv, relay_send, relay_recv, out_sem):
    outer_size, far_size, chunks, rows = sizes
    patch, rank = lax.axis_index("patch"), lax.axis_index("hidden")
    outer, inner = patch // 2, patch % 2
    far, side = rank // 2, rank % 2
    pair_peer = outer * 2 + (1 - inner)
    side_peer = far * 2 + (1 - side)
    shift = lambda at, by, size: lax.rem(at + by, size)
    cross_peers = [shift(outer, k + 1, outer_size) * 2 + inner for k in range(outer_size - 1)]
    far_peers = [shift(far, k + 1, far_size) * 2 + side for k in range(far_size - 1)]
    blocks = [shift(outer, k + 1, outer_size) for k in range(outer_size)]

    barrier = pltpu.get_barrier_semaphore()
    for peer in [pair_peer] + cross_peers:
        pl.semaphore_signal(barrier, inc=1, device_id={"patch": peer}, device_id_type=pl.DeviceIdType.MESH)
    for peer in [side_peer] + far_peers:
        pl.semaphore_signal(barrier, inc=1, device_id={"hidden": peer}, device_id_type=pl.DeviceIdType.MESH)
    pl.semaphore_wait(barrier, outer_size + far_size)

    def send(src, dst, send_sem, recv_sem, axis, peer):
        copy = pltpu.make_async_remote_copy(
            src_ref=src,
            dst_ref=dst,
            send_sem=send_sem,
            recv_sem=recv_sem,
            device_id={axis: peer},
            device_id_type=pl.DeviceIdType.MESH,
        )
        copy.start()
        return copy

    def span(c):
        return pl.ds(c * rows, rows)

    loads, pairs, crosses, sides, fars, relays, outs = [], {}, {}, {}, {}, {}, []
    tile = row_block(rows, 128)

    def load(c):
        copy = pltpu.make_async_copy(part_ref.at[:, :, span(c)], stage.at[c % 2], own_sem.at[c])
        copy.start()
        loads.append(copy)

    load(0)
    load(1)
    for c in range(chunks):
        loads[c].wait()

        def narrow(i, carry):
            at = pl.ds(pl.multiple_of(i * tile, tile), tile)
            for block in range(outer_size):
                own[c, block, at] = stage[c % 2, block, inner, at].astype(jnp.bfloat16)
                leaving[c, block, at] = stage[c % 2, block, 1 - inner, at].astype(jnp.bfloat16)
            return carry

        lax.fori_loop(0, rows // tile, narrow, 0)
        if c + 2 < chunks:
            load(c + 2)
        for k in range(outer_size):
            pairs[c, k] = send(
                leaving.at[c, blocks[k]],
                paired.at[c, k],
                pair_send.at[c, k],
                pair_recv.at[c, k],
                "patch",
                pair_peer,
            )

    def reduce_pair(c):
        for k in range(outer_size - 1):
            pairs[c, k].wait_recv()

            def add(i, carry):
                at = pl.ds(pl.multiple_of(i * tile, tile), tile)
                total = own[c, blocks[k], at].astype(jnp.float32) + paired[c, k, at].astype(jnp.float32)
                own[c, blocks[k], at] = total.astype(jnp.bfloat16)
                return carry

            lax.fori_loop(0, rows // tile, add, 0)
            crosses[c, k] = send(
                own.at[c, blocks[k]],
                crossed.at[c, k],
                cross_send.at[c, k],
                cross_recv.at[c, k],
                "patch",
                cross_peers[k],
            )
        pairs[c, outer_size - 1].wait_recv()

    def emit(c, source, sem):
        copy = pltpu.make_async_copy(gathered.at[c, source], out_ref.at[source, span(c)], sem)
        copy.start()
        outs.append(copy)

    def finish(c):
        for k in range(outer_size - 1):
            crosses[c, k].wait_recv()

        def add(i, carry):
            at = pl.ds(pl.multiple_of(i * tile, tile), tile)
            total = own[c, outer, at].astype(jnp.float32) + paired[c, outer_size - 1, at].astype(jnp.float32)
            for k in range(outer_size - 1):
                total = total + crossed[c, k, at].astype(jnp.float32)
            gathered[c, rank, at] = total.astype(jnp.bfloat16)
            return carry

        lax.fori_loop(0, rows // tile, add, 0)
        mine = gathered.at[c, rank]
        for k in range(far_size - 1):
            fars[c, k] = send(mine, mine, far_send.at[c, k], far_recv.at[c, k], "hidden", far_peers[k])
        sides[c] = send(mine, mine, side_send.at[c], side_recv.at[c], "hidden", side_peer)
        emit(c, rank, out_sem.at[c, 0])

    def relay(c):
        for k in range(far_size - 1):
            fars[c, k].wait_recv()
            source = shift(far, far_size - 1 - k, far_size) * 2 + side
            block = gathered.at[c, source]
            relays[c, k] = send(block, block, relay_send.at[c, k], relay_recv.at[c, k], "hidden", side_peer)
            emit(c, source, out_sem.at[c, 1 + k])

    def collect(c):
        sides[c].wait_recv()
        emit(c, side_peer, out_sem.at[c, far_size])
        for k in range(far_size - 1):
            relays[c, k].wait_recv()
            source = shift(far, far_size - 1 - k, far_size) * 2 + (1 - side)
            emit(c, source, out_sem.at[c, far_size + 1 + k])

    for c in range(chunks + 3):
        if c < chunks:
            reduce_pair(c)
        if 0 <= c - 1 < chunks:
            finish(c - 1)
        if 0 <= c - 2 < chunks:
            relay(c - 2)
        if 0 <= c - 3 < chunks:
            collect(c - 3)
    for group in (pairs, crosses, sides, fars, relays):
        for copy in group.values():
            copy.wait_send()
    for copy in outs:
        copy.wait()


def combine(parts, patches, ranks):
    total_rows, width = parts.shape
    rows = total_rows // patches
    outer_size, far_size = patches // 2, ranks // 2
    chunks = 10 if rows % 160 == 0 else 4
    size = rows // chunks
    dma = pltpu.SemaphoreType.DMA
    cross = (chunks, outer_size - 1)
    far = (chunks, far_size - 1)
    return pl.pallas_call(
        functools.partial(combine_kernel, (outer_size, far_size, chunks, size)),
        in_specs=[pl.BlockSpec(memory_space=pl.ANY)],
        out_specs=pl.BlockSpec(memory_space=pl.ANY),
        out_shape=jax.ShapeDtypeStruct((ranks, rows, width), jnp.bfloat16),
        scratch_shapes=[
            pltpu.VMEM((2, outer_size, 2, size, width), jnp.float32),
            pltpu.VMEM((chunks, outer_size, size, width), jnp.bfloat16),
            pltpu.VMEM((chunks, outer_size, size, width), jnp.bfloat16),
            pltpu.VMEM((chunks, outer_size, size, width), jnp.bfloat16),
            pltpu.VMEM(cross + (size, width), jnp.bfloat16),
            pltpu.VMEM((chunks, ranks, size, width), jnp.bfloat16),
            dma((chunks,)),
            dma((chunks, outer_size)),
            dma((chunks, outer_size)),
            dma(cross),
            dma(cross),
            dma((chunks,)),
            dma((chunks,)),
            dma(far),
            dma(far),
            dma(far),
            dma(far),
            dma((chunks, ranks)),
        ],
        compiler_params=pltpu.CompilerParams(
            collective_id=0, has_side_effects=True, vmem_limit_bytes=48 * 1024 * 1024
        ),
        name="combine",
    )(parts.reshape(outer_size, 2, rows, width))


def pieces(x, size):
    return [x] + [
        lax.ppermute(x, "hidden", [((j + k) % size, j) for j in range(size)]) for k in range(1, size)
    ]


def rows_at(x, index):
    return x.at[index].get(mode="promise_in_bounds")


def turned(x, shift, axis):
    return lax.dynamic_slice_in_dim(jnp.concatenate([x, x], axis), shift, x.shape[axis], axis)


def shards(
    patches,
    hidden_size,
    grid_latent,
    mesh_latent,
    edge_latent,
    senders,
    receivers,
    mesh_slot,
    edge_counts,
    w_edge,
    w_sender,
    w_receiver,
    edge_bias,
    w_edge_out,
    edge_out_bias,
    edge_gain,
    edge_shift,
    w_mesh_in,
    w_message_in,
    mesh_bias,
    w_mesh_out,
    mesh_out_bias,
    mesh_gain,
    mesh_shift,
):
    patch_index = lax.axis_index("patch")
    column_index = lax.axis_index("hidden")
    own_grid = grid_latent.shape[0]
    own_edges = edge_latent.shape[0]
    width = w_edge.shape[1]
    full = w_edge.shape[0]
    mesh_total = mesh_slot.shape[0]
    column = jnp.stack([column_index.astype(jnp.int32), edge_counts[0]])

    receiver_part = jnp.dot(mesh_latent, w_receiver, preferred_element_type=jnp.float32).astype(
        jnp.bfloat16
    )
    table = lax.all_gather(receiver_part, "patch", axis=0, tiled=True)

    outer = pieces(jnp.concatenate([w_edge_out, w_mesh_out], 0), hidden_size)
    inner = pieces(jnp.concatenate([w_mesh_in, w_message_in], 0), hidden_size)
    biases = jnp.concatenate(pieces(jnp.stack([edge_out_bias, mesh_bias, mesh_out_bias]), hidden_size), 1)
    to_first = lax.rem(hidden_size - column_index, hidden_size)
    edge_w_out = jnp.concatenate([part[:width] for part in outer], 0)
    edge_w_out = turned(turned(edge_w_out, to_first * width, 0), column_index * width, 1)
    mesh_w_out = turned(jnp.concatenate([part[width:] for part in outer], 0), column_index * width, 1)
    mesh_w_in = jnp.concatenate([part[:full] for part in inner], 1)
    mesh_w_msg = jnp.concatenate([part[full:] for part in inner], 1)

    target_rows = rows_at(mesh_slot, receivers)
    weights = (edge_w_out, mesh_w_out, mesh_w_in, mesh_w_msg, biases)
    target_rows, weights = lax.optimization_barrier((target_rows, weights))
    edge_w_out, mesh_w_out, mesh_w_in, mesh_w_msg, biases = weights
    sender_local = senders - patch_index * own_grid
    sender_part = jnp.dot(grid_latent, w_sender, preferred_element_type=jnp.float32)
    sent = rows_at(sender_part, sender_local)

    step = own_edges // CHUNKS
    spread_sums = jnp.zeros((mesh_total, width), jnp.float32)
    edge_outs = []
    for at in range(0, own_edges, step):
        rows = slice(at, at + step)
        edge_pre = (
            jnp.dot(edge_latent[rows], w_edge, preferred_element_type=jnp.float32)
            + sent[rows]
            + rows_at(table, target_rows[rows]).astype(jnp.float32)
            + edge_bias
        )
        edge_hidden = jax.nn.silu(edge_pre).astype(jnp.bfloat16)
        gathered_hidden = lax.all_gather(edge_hidden, "hidden", axis=1, tiled=True)
        message, edge_out = edge_finish(
            column,
            gathered_hidden,
            edge_latent,
            at,
            edge_w_out,
            biases[:1],
            edge_gain[None],
            edge_shift[None],
        )
        edge_outs.append(edge_out)
        spread_sums = spread_sums.at[target_rows[rows]].add(message, mode="promise_in_bounds")
    edge_out = jnp.concatenate(edge_outs, 0)

    if width % 128 == 0 and patches % 2 == 0 and patches > 2 and hidden_size % 2 == 0 and hidden_size > 2:
        gathered = combine(spread_sums, patches, hidden_size)
    else:
        received = lax.psum_scatter(
            spread_sums.astype(jnp.bfloat16), "patch", scatter_dimension=0, tiled=True
        )
        gathered = lax.all_gather(received, "hidden", axis=1, tiled=True)[None]
    mesh_out = mesh_finish(
        column,
        mesh_latent,
        gathered,
        mesh_w_in,
        mesh_w_msg,
        biases[1:2],
        mesh_w_out,
        biases[2:3],
        mesh_gain[None],
        mesh_shift[None],
    )
    return (mesh_out, edge_out)


def solution(mesh):
    return jax.shard_map(
        functools.partial(shards, mesh.shape["patch"], mesh.shape["hidden"]),
        mesh=mesh,
        in_specs=(
            P("patch", None),
            P("patch", None),
            P("patch", None),
            P("patch"),
            P("patch"),
            P(),
            P("patch"),
            P(None, "hidden"),
            P(None, "hidden"),
            P(None, "hidden"),
            P("hidden"),
            P("hidden", None),
            P("hidden"),
            P("hidden"),
            P("hidden"),
            P(None, "hidden"),
            P(None, "hidden"),
            P("hidden"),
            P("hidden", None),
            P("hidden"),
            P("hidden"),
            P("hidden"),
        ),
        out_specs=(P("patch", "hidden"), P("patch", "hidden")),
        check_vma=False,
    )
```

profile of v0, /device:TPU:1, one launch (start us, length us, event | category | flops | bytes accessed | tf_op | source)
XLA Modules:
  0.0 459.1 jit_solution(11043513995759359585)
XLA Ops:
  7.3 5.2 %convolution_convert_fusion = bf16[5120,128]{1,0:T(8,128)(2,1)} fusion(bf16[5120,512]{1,0:T(8,128)(2,1)} %own_ref.1, bf16[512,128]{1,0:T(8,128)(2,1)} %param.31), kind=kOutput, calls=%fused_computation.8 | convolution fusion | flops 671744000 | bytes 6684672 | tf_op jit(solution)/shard_map/dot_general | solution.py:359
  12.6 2.6 collective-permute-start.8
  16.4 1.6 constant_dynamic-update-slice_fusion.4
  19.9 1.6 constant_dynamic-update-slice_fusion
  21.7 3.1 fusion.29
  24.8 45.5 %gather_fusion = s32[8192]{0:T(1024)S(1)} fusion(s32[40960]{0:T(1024)S(1)} %copy-done.3, s32[8192]{0:T(1024)S(1)} %fusion.20), kind=kCustom, calls=%fused_computation | custom fusion | bytes 98304 | tf_op jit(solution)/shard_map/gather | solution.py:317
  70.4 27.7 %gather_fusion.1 = f32[8192,128]{1,0:T(8,128)} fusion(f32[3072,128]{1,0:T(8,128)S(1)} %copy-done.4, s32[8192]{0:T(1024)S(1)} %fusion.21), kind=kCustom, calls=%fused_computation.1 | custom fusion | bytes 8421376 | tf_op jit(solution)/shard_map/gather | solution.py:317
  100.1 1.5 collective-permute-start.1
  102.9 7.8 %collective-permute-done.1 = bf16[256,512]{1,0:T(8,128)(2,1)S(1)} collective-permute-done((bf16[256,512]{1,0:T(8,128)(2,1)}, bf16[256,512]{1,0:T(8,128)(2,1)S(1)}, u32[]{:S(2)}, u32[]{:S(2)}) %collective-permute-start.1) | collective-permute-done | bytes 262176 | tf_op jit(solution)/shard_map/ppermute | solution.py:312
  110.7 5.6 %collective-permute-done.2 = bf16[256,512]{1,0:T(8,128)(2,1)S(1)} collective-permute-done((bf16[256,512]{1,0:T(8,128)(2,1)}, bf16[256,512]{1,0:T(8,128)(2,1)S(1)}, u32[]{:S(2)}, u32[]{:S(2)}) %collective-permute-start.2) | collective-permute-done | bytes 262176 | tf_op jit(solution)/shard_map/ppermute | solution.py:312
  119.6 3.0 fusion.15
  122.6 41.9 %all-gather.4.cloned.1.call-done = bf16[40960,128]{1,0:T(8,128)(2,1)} async-done(((bf16[5120,128]{1,0:T(8,128)(2,1)}), bf16[40960,128]{1,0:T(8,128)(2,1)}) %all-gather.4.cloned.1.call-update) | async-done | bytes 10485776 | tf_op jit(solution)/shard_map/all_gather | solution.py:362
  164.6 16.4 %gather_fusion.2 = bf16[4096,128]{1,0:T(8,128)(2,1)S(1)} fusion(bf16[40960,128]{1,0:T(8,128)(2,1)} %all-gather.4.cloned.1.call-done, s32[4096]{0:T(1024)S(1)} %get-tuple-element.37), kind=kCustom, calls=%fused_computation.2 | custom fusion | bytes 2113536 | tf_op jit(solution)/shard_map/gather | solution.py:317
  181.0 5.1 %multiply_convert_fusion.1 = bf16[4096,128]{1,0:T(8,128)(2,1)} fusion(f32[8192,128]{1,0:T(8,128)} %gather_fusion.1, bf16[512,128]{1,0:T(8,128)(2,1)S(1)} %copy-done.18, bf16[8192,512]{1,0:T(8,128)(2,1)} %latent_ref.4, bf16[4096,128]{1,0:T(8,128)(2,1)S(1)} %gather_fusion.2, f32[128]{0:T(128)S(1)} %copy-done.19), kind=kOutput, calls=%fused_computation.19 | convolution fusion | flops 541589504 | bytes 8520192 | tf_op jit(solution)/shard_map/dot_general | solution.py:388
  186.3 16.4 %gather_fusion.3 = bf16[4096,128]{1,0:T(8,128)(2,1)S(1)} fusion(bf16[40960,128]{1,0:T(8,128)(2,1)} %all-gather.4.cloned.1.call-done, s32[4096]{0:T(1024)S(1)} %get-tuple-element.36), kind=kCustom, calls=%fused_computation.3 | custom fusion | bytes 2113536 | tf_op jit(solution)/shard_map/gather | solution.py:317
  202.7 5.1 %multiply_convert_fusion = bf16[4096,128]{1,0:T(8,128)(2,1)} fusion(f32[8192,128]{1,0:T(8,128)} %gather_fusion.1, bf16[512,128]{1,0:T(8,128)(2,1)S(1)} %copy-done.18, bf16[8192,512]{1,0:T(8,128)(2,1)} %latent_ref.4, bf16[4096,128]{1,0:T(8,128)(2,1)S(1)} %gather_fusion.3, f32[128]{0:T(128)S(1)} %copy-done.19), kind=kOutput, calls=%fused_computation.18 | convolution fusion | flops 541589504 | bytes 8520192 | tf_op jit(solution)/shard_map/dot_general | solution.py:388
  209.7 10.8 %all-gather.6.cloned.1.call-done.hidden_ref = bf16[4096,512]{1,0:T(8,128)(2,1)} async-done(((bf16[4096,128]{1,0:T(8,128)(2,1)}), bf16[4096,512]{1,0:T(8,128)(2,1)}) %all-gather.6.cloned.1.call-update) | async-done | bytes 4194320 | tf_op jit(solution)/shard_map/all_gather | solution.py:394
  220.6 8.0 %edge_finish.2 = (f32[4096,128]{1,0:T(8,128)}, bf16[4096,128]{1,0:T(8,128)(2,1)}) custom-call(s32[2]{0:T(128)} %pad_add_fusion.scalars.column, bf16[4096,512]{1,0:T(8,128)(2,1)} %all-gather.6.cloned.1.call-done.hidden_ref, bf16[8192,512]{1,0:T(8,128)(2,1)} %latent_ref.4, bf16[512,512]{1,0:T(8,128)(2,1)} %get-tuple-element.13.w_ref, ...), custom_call_target="tpu_custom_call" | custom-call | flops 2147483648 | bytes 8388608 | tf_op jit(solution)/shard_map/edge_finish/pallas_call | solution.py:53
  228.5 31.1 %scatter_custom_fusion = f32[40960,128]{1,0:T(8,128)} fusion(s32[4096]{0:T(1024)S(1)} %get-tuple-element.39, f32[4096,128]{1,0:T(8,128)} %get-tuple-element.15, f32[]{:T(128)} %constant.13.clone.1), kind=kCustom, calls=%fused_computation.6 | custom fusion | flops 524288 | bytes 20972032 | tf_op jit(solution)/shard_map/scatter-add | solution.py:406
  259.6 8.0 %edge_finish.3 = (f32[4096,128]{1,0:T(8,128)}, bf16[4096,128]{1,0:T(8,128)(2,1)}) custom-call(s32[2]{0:T(128)} %pad_add_fusion.scalars.column, bf16[4096,512]{1,0:T(8,128)(2,1)} %all-gather.8.cloned.1.call-done.hidden_ref, bf16[8192,512]{1,0:T(8,128)(2,1)} %latent_ref.4, bf16[512,512]{1,0:T(8,128)(2,1)} %get-tuple-element.13.w_ref, ...), custom_call_target="tpu_custom_call" | custom-call | flops 2147483648 | bytes 8388608 | tf_op jit(solution)/shard_map/edge_finish/pallas_call | solution.py:53
  267.6 34.4 %scatter_fusion = f32[40960,128]{1,0:T(8,128)} fusion(f32[40960,128]{1,0:T(8,128)} %scatter_custom_fusion, s32[4096]{0:T(1024)S(1)} %get-tuple-element.38, f32[4096,128]{1,0:T(8,128)} %get-tuple-element.16), kind=kCustom, calls=%fused_computation.5 | custom fusion | flops 524288 | bytes 6307840 | tf_op jit(solution)/shard_map/scatter-add | solution.py:406
  302.0 132.2 %combine.1.summed_ref = bf16[4,5120,128]{2,1,0:T(8,128)(2,1)S(1)} custom-call(f32[4,2,5120,128]{3,2,1,0:T(8,128)} %bitcast.15), custom_call_target="tpu_custom_call" | custom-call | tf_op jit(solution)/shard_map/combine/pallas_call | solution.py:278
  434.2 2.3 copy-done.2
  438.0 14.6 %mesh_finish.1 = bf16[5120,128]{1,0:T(8,128)(2,1)} custom-call(s32[2]{0:T(128)} %pad_add_fusion.scalars.column, bf16[5120,512]{1,0:T(8,128)(2,1)} %own_ref.1, bf16[5120,512]{1,0:T(8,128)(2,1)} %own_ref.1, bf16[4,5120,128]{2,1,0:T(8,128)(2,1)} %copy-done.2, bf16[512,512]{1,0:T(8,128)(2,1)} %get-tuple-element.17.w_in_ref, ...), custom_call_target="tpu_custom_call" | custom-call | flops 8053063680 | bytes 13107200 | tf_op jit(solution)/shard_map/mesh_finish/pallas_call | solution.py:98
  (82 shorter events, 13.0 us)
Async XLA Ops:
  7.2 14.5 %copy-start = (bf16[3072,512]{1,0:T(8,128)(2,1)S(1)}, bf16[3072,512]{1,0:T(8,128)(2,1)}, u32[]{:S(2)}) copy-start(bf16[3072,512]{1,0:T(8,128)(2,1)} %param.22) | copy-start | bytes 9437188
  7.2 5.4 %copy-start.15 = (f32[128]{0:T(128)S(1)}, f32[128]{0:T(128)}, u32[]{:S(2)}) copy-start(f32[128]{0:T(128)} %param.41) | copy-start | bytes 1540
  7.2 8.5 %copy-start.8 = (bf16[512,128]{1,0:T(8,128)(2,1)S(1)}, bf16[512,128]{1,0:T(8,128)(2,1)}, u32[]{:S(2)}) copy-start(bf16[512,128]{1,0:T(8,128)(2,1)} %param.37) | copy-start | bytes 393220
  7.2 12.0 %copy-start.7 = (bf16[128,512]{1,0:T(8,128)(2,1)S(1)}, bf16[128,512]{1,0:T(8,128)(2,1)}, u32[]{:S(2)}) copy-start(bf16[128,512]{1,0:T(8,128)(2,1)} %param.33) | copy-start | bytes 393220
  7.2 157.3 %all-gather.4.cloned.1.call-start = ((), (), s32[]{:S(2)}) async-start(), calls=%async_computation | async-start | bytes 11796480 | tf_op jit(solution)/shard_map/all_gather | solution.py:362
  12.5 9.1 %copy-start.13 = (s32[8192]{0:T(1024)S(1)}, s32[8192]{0:T(1024)}, u32[]{:S(2)}) copy-start(s32[8192]{0:T(1024)} %param.26) | copy-start | bytes 98308
  12.5 208.0 %all-gather.6.cloned.1.call-start = ((), (), s32[]{:S(2)}) async-start(), calls=%async_computation.1 | async-start | bytes 5242880 | tf_op jit(solution)/shard_map/all_gather | solution.py:394
  12.6 85.5 %collective-permute-start.8 = (f32[3,128]{1,0:T(4,128)S(1)}, f32[3,128]{1,0:T(4,128)S(1)}, u32[]{:S(2)}, u32[]{:S(2)}) collective-permute-start(f32[3,128]{1,0:T(4,128)S(1)} %pad_maximum_fusion.4), channel_id=1, source_target_pairs={{3,0},{0,1},{1,2},{2,3},{7,4},{4,5},{5,6},{6,7},{11,8},{8,9},{9,10... | collective-permute-start | bytes 4616 | tf_op jit(solution)/shard_map/ppermute | solution.py:312
  15.3 84.2 %collective-permute-start.7 = (f32[3,128]{1,0:T(4,128)S(1)}, f32[3,128]{1,0:T(4,128)S(1)}, u32[]{:S(2)}, u32[]{:S(2)}) collective-permute-start(f32[3,128]{1,0:T(4,128)S(1)} %pad_maximum_fusion.4), channel_id=1, source_target_pairs={{2,0},{3,1},{0,2},{1,3},{6,4},{7,5},{4,6},{5,7},{10,8},{11,9},{8,1... | collective-permute-start | bytes 4616 | tf_op jit(solution)/shard_map/ppermute | solution.py:312
  15.3 84.9 %collective-permute-start.6 = (f32[3,128]{1,0:T(4,128)S(1)}, f32[3,128]{1,0:T(4,128)S(1)}, u32[]{:S(2)}, u32[]{:S(2)}) collective-permute-start(f32[3,128]{1,0:T(4,128)S(1)} %pad_maximum_fusion.4), channel_id=1, source_target_pairs={{1,0},{2,1},{3,2},{0,3},{5,4},{6,5},{7,6},{4,7},{9,8},{10,9},{11,1... | collective-permute-start | bytes 4616 | tf_op jit(solution)/shard_map/ppermute | solution.py:312
  18.0 99.4 %collective-permute-start.5 = (bf16[1024,128]{1,0:T(8,128)(2,1)}, bf16[1024,128]{1,0:T(8,128)(2,1)}, u32[]{:S(2)}, u32[]{:S(2)}) collective-permute-start(bf16[1024,128]{1,0:T(8,128)(2,1)} %constant_dynamic-update-slice_fusion.4), channel_id=1, source_target_pairs={{3,0},{0,1},{1,2},{2,3},{7,4},{4,5},{5,6},{6,7},{11,8},{8,9},{9,10... | collective-permute-start | bytes 786440 | tf_op jit(solution)/shard_map/ppermute | solution.py:312
  21.5 80.1 %collective-permute-start = (bf16[256,512]{1,0:T(8,128)(2,1)}, bf16[256,512]{1,0:T(8,128)(2,1)}, u32[]{:S(2)}, u32[]{:S(2)}) collective-permute-start(bf16[256,512]{1,0:T(8,128)(2,1)} %constant_dynamic-update-slice_fusion), channel_id=1, source_target_pairs={{1,0},{2,1},{3,2},{0,3},{5,4},{6,5},{7,6},{4,7},{9,8},{10,9},{11,1... | collective-permute-start | bytes 786440 | tf_op jit(solution)/shard_map/ppermute | solution.py:312
  24.8 45.6 %copy-start.4 = (f32[3072,128]{1,0:T(8,128)S(1)}, f32[3072,128]{1,0:T(8,128)}, u32[]{:S(2)}) copy-start(f32[3072,128]{1,0:T(8,128)} %fusion.29) | copy-start | bytes 4718596
  70.4 31.5 %copy-start.12 = (bf16[1024,512]{1,0:T(8,128)(2,1)S(1)}, bf16[1024,512]{1,0:T(8,128)(2,1)}, u32[]{:S(2)}) copy-start(bf16[1024,512]{1,0:T(8,128)(2,1)} %get-tuple-element.35) | copy-start | bytes 3145732
  98.1 20.3 %collective-permute-start.4 = (bf16[1024,128]{1,0:T(8,128)(2,1)}, bf16[1024,128]{1,0:T(8,128)(2,1)S(1)}, u32[]{:S(2)}, u32[]{:S(2)}) collective-permute-start(bf16[1024,128]{1,0:T(8,128)(2,1)} %constant_dynamic-update-slice_fusion.4), channel_id=1, source_target_pairs={{2,0},{3,1},{0,2},{1,3},{6,4},{7,5},{4,6},{5,7},{10,8},{11,9},{8,1... | collective-permute-start | bytes 786440 | tf_op jit(solution)/shard_map/ppermute | solution.py:312
  99.5 19.0 %collective-permute-start.3 = (bf16[1024,128]{1,0:T(8,128)(2,1)}, bf16[1024,128]{1,0:T(8,128)(2,1)S(1)}, u32[]{:S(2)}, u32[]{:S(2)}) collective-permute-start(bf16[1024,128]{1,0:T(8,128)(2,1)} %constant_dynamic-update-slice_fusion.4), channel_id=1, source_target_pairs={{1,0},{2,1},{3,2},{0,3},{5,4},{6,5},{7,6},{4,7},{9,8},{10,9},{11,1... | collective-permute-start | bytes 786440 | tf_op jit(solution)/shard_map/ppermute | solution.py:312
  100.1 10.5 %collective-permute-start.1 = (bf16[256,512]{1,0:T(8,128)(2,1)}, bf16[256,512]{1,0:T(8,128)(2,1)S(1)}, u32[]{:S(2)}, u32[]{:S(2)}) collective-permute-start(bf16[256,512]{1,0:T(8,128)(2,1)} %constant_dynamic-update-slice_fusion), channel_id=1, source_target_pairs={{2,0},{3,1},{0,2},{1,3},{6,4},{7,5},{4,6},{5,7},{10,8},{11,9},{8,1... | collective-permute-start | bytes 786440 | tf_op jit(solution)/shard_map/ppermute | solution.py:312
  101.6 14.7 %collective-permute-start.2 = (bf16[256,512]{1,0:T(8,128)(2,1)}, bf16[256,512]{1,0:T(8,128)(2,1)S(1)}, u32[]{:S(2)}, u32[]{:S(2)}) collective-permute-start(bf16[256,512]{1,0:T(8,128)(2,1)} %constant_dynamic-update-slice_fusion), channel_id=1, source_target_pairs={{3,0},{0,1},{1,2},{2,3},{7,4},{4,5},{5,6},{6,7},{11,8},{8,9},{9,10... | collective-permute-start | bytes 786440 | tf_op jit(solution)/shard_map/ppermute | solution.py:312
  164.6 16.4 %copy-start.18 = (bf16[512,128]{1,0:T(8,128)(2,1)S(1)}, bf16[512,128]{1,0:T(8,128)(2,1)}, u32[]{:S(2)}) copy-start(bf16[512,128]{1,0:T(8,128)(2,1)} %param.29) | copy-start | bytes 393220
  164.6 16.4 %copy-start.19 = (f32[128]{0:T(128)S(1)}, f32[128]{0:T(128)}, u32[]{:S(2)}) copy-start(f32[128]{0:T(128)} %param.32) | copy-start | bytes 1540
  186.1 73.5 %all-gather.8.cloned.1.call-start = ((), (), s32[]{:S(2)}) async-start(), calls=%async_computation.2 | async-start | bytes 5242880 | tf_op jit(solution)/shard_map/all_gather | solution.py:394
  302.0 134.6 %copy-start.5 = (bf16[4096,128]{1,0:T(8,128)(2,1)S(1)}, bf16[4096,128]{1,0:T(8,128)(2,1)}, u32[]{:S(2)}) copy-start(bf16[4096,128]{1,0:T(8,128)(2,1)} %get-tuple-element.20) | copy-start | bytes 3145732
  302.0 134.6 %copy-start.6 = (bf16[4096,128]{1,0:T(8,128)(2,1)S(1)}, bf16[4096,128]{1,0:T(8,128)(2,1)}, u32[]{:S(2)}) copy-start(bf16[4096,128]{1,0:T(8,128)(2,1)} %get-tuple-element.21) | copy-start | bytes 3145732
  438.0 14.6 %copy-start.1 = (bf16[3072,512]{1,0:T(8,128)(2,1)S(1)}, bf16[3072,512]{1,0:T(8,128)(2,1)}, u32[]{:S(2)}) copy-start(bf16[3072,512]{1,0:T(8,128)(2,1)} %param.22) | copy-start | bytes 9437188
  (8 other events, 25.1 us)
Sparse Core Ops, SparseCore 0:
  12.7 151.8 all-gather.3
  186.2 34.2 all-gather.5
  222.1 34.9 all-gather.7
where the time goes:
time: 460 us; the launch traced here: 459 us
  Pallas kernels  163 us (35%)
  local copies, waits for them, and re-layouts  117 us (25%)
  other arithmetic  71.7 us (16%)
  waiting for transfers between devices  66.2 us (14%)
  matrix products  18.5 us (4%)
  between operations  14.7 us (3%)
  starting transfers between devices  8.58 us (2%)
    pallas_call x1, Pallas kernels, combine(): pl.pallas_call(functools.partial(combine_kernel, (outer_size, far_size, c...  132 us
    gather x4, local copies, waits for them, and re-layouts, rows_at(): return x.at[index].get(mode='promise_in_bounds')  106 us
    scatter-add x2, other arithmetic, shards(): spread_sums.at[target_rows[rows]].add(message, mode='promise_in_bounds')  65.5 us
    all_gather x1, waiting for transfers between devices, shards(): table = lax.all_gather(receiver_part, 'patch', axis=0, tiled=True)  41.9 us
    pallas_call x2, Pallas kernels, edge_finish(): pl.pallas_call(functools.partial(edge_kernel, first_row), grid_spec=pltpu...  15.9 us
    pallas_call x1, Pallas kernels, mesh_finish(): pl.pallas_call(mesh_kernel, grid_spec=pltpu.PrefetchScalarGridSpec(num_sc...  14.6 us
    ppermute x9, waiting for transfers between devices, pieces(): lax.ppermute(x, 'hidden', [((j + k) % size, j) for j in range(size)])  13.4 us
    all_gather x2, waiting for transfers between devices, shards(): gathered_hidden = lax.all_gather(edge_hidden, 'hidden', axis=1, tiled=True)  10.8 us
  transfers between devices with their start and end apart: 12, of which 4 were waited for; matrix products, arithmetic and copies ran while one was open for 31% of the time, Pallas kernels for 2%

commit v1 on v0

v1 whole, which is shorter than its diff:
```python
import functools

import jax
import jax.numpy as jnp
from jax import lax
from jax.experimental import pallas as pl
from jax.experimental.pallas import tpu as pltpu
from jax.sharding import PartitionSpec as P

EPSILON = 1e-05
CHUNK = 256
OWN_CHUNKS = 3
NEAR_CHUNKS = 2
FAR_ROWS = 192
CLASS_ROWS = 8


def iota(shape, axis):
    return lax.broadcasted_iota(jnp.int32, shape, axis)


def one_hot(cond):
    return jnp.where(cond, 1.0, 0.0).astype(jnp.bfloat16)


def dot(a, b):
    return jnp.dot(a, b, preferred_element_type=jnp.float32)


def dot_nt(a, b):
    return lax.dot_general(a, b, (((1,), (1,)), ((), ())), preferred_element_type=jnp.float32)


def wide(block):
    return jnp.concatenate([block[j : j + 1, :] for j in range(block.shape[0])], axis=1)


def normalize(total, gain, offset):
    width = total.shape[1]
    center = jnp.sum(total, axis=1, keepdims=True) / width
    centered = total - center
    spread = jnp.sum(centered * centered, axis=1, keepdims=True) / width
    return centered * lax.rsqrt(spread + EPSILON) * gain + offset


def class_plan(patches):
    starts = [0, OWN_CHUNKS] + [OWN_CHUNKS + 2 * NEAR_CHUNKS + k - 2 for k in range(2, patches - 1)]
    starts.append(OWN_CHUNKS + NEAR_CHUNKS)
    caps = [OWN_CHUNKS * CHUNK, NEAR_CHUNKS * CHUNK] + [FAR_ROWS] * (patches - 3) + [NEAR_CHUNKS * CHUNK]
    return starts, caps, OWN_CHUNKS + 2 * NEAR_CHUNKS + patches - 3


def index_kernel(sizes, where_am_i, recv_ref, send_ref, table_ref, req_ref, edge_ref, send_out_ref, where_ref, target, masks, position, local, totals):
    patches, ranks, mesh_rows, parts = sizes
    groups = recv_ref.shape[0]
    own_rows = mesh_rows // ranks
    starts, caps, chunks = class_plan(patches)
    high = table_ref.shape[1]
    me, rank_me, count = where_am_i[0], where_am_i[1], where_am_i[2]

    def lookup(i, carry):
        row = wide(recv_ref[pl.ds(i * 8, 8), :])
        hot = one_hot(iota((high, 1024), 0) == (row >> 7))
        found = dot(table_ref[...], hot)
        low = iota((128, 1024), 0) == (row & 127)
        value = jnp.zeros((1, 1024), jnp.float32)
        for part in range(parts):
            piece = jnp.where(low, found[part * 128 : (part + 1) * 128], 0.0)
            value = value + float(256**part) * jnp.sum(piece, axis=0, keepdims=True)
        value = value.astype(jnp.int32)
        block = jnp.concatenate([value[:, j * 128 : (j + 1) * 128] for j in range(8)], axis=0)
        target[pl.ds(i * 8, 8), :] = block
        return carry

    lax.fori_loop(0, groups // 8, lookup, 0)

    shape = (groups, 128)
    goal = target[...]
    owner = sum((goal >= k * mesh_rows).astype(jnp.int32) for k in range(1, patches))
    inside = goal - owner * mesh_rows
    part = sum((inside >= k * own_rows).astype(jnp.int32) for k in range(1, ranks))
    offset = owner - me
    offset = jnp.where(offset < 0, offset + patches, offset)
    slot = iota(shape, 0) * 128 + iota(shape, 1)
    live = slot < count
    label = jnp.where(live, offset * ranks + part, -1)
    classes = patches * ranks
    for c in range(classes):
        masks[c * groups : (c + 1) * groups, :] = one_hot(label == c)
    steps = jnp.concatenate([one_hot(iota((128, 128), 0) <= iota((128, 128), 1)), jnp.ones((128, 128), jnp.bfloat16)], axis=1)
    totals[...] = dot(masks[...], steps)
    below = one_hot(iota((groups, groups), 1) < iota((groups, groups), 0))
    rank = jnp.zeros(shape, jnp.float32)
    over = jnp.zeros((1, 128), jnp.float32)
    for c in range(classes):
        block = totals[c * groups : (c + 1) * groups, :]
        inner, whole = block[:, :128], block[:, 128:]
        before = dot(below, whole.astype(jnp.bfloat16))
        mine = jnp.where(label == c, 1.0, 0.0)
        rank = rank + mine * (inner - 1.0 + before)
        full = before[groups - 1 :, :] + whole[groups - 1 :, :]
        over = jnp.maximum(over, jnp.where(full > float(caps[c // ranks]), 1.0, 0.0))
    rank = rank.astype(jnp.int32)
    first = jnp.zeros(shape, jnp.int32)
    cap = jnp.zeros(shape, jnp.int32)
    for k in range(patches):
        first = jnp.where(offset == k, starts[k] * CHUNK, first)
        cap = jnp.where(offset == k, caps[k], cap)
    spot = part * (chunks * CHUNK) + first + rank
    spot = jnp.minimum(spot, ranks * chunks * CHUNK - 1)
    where_ref[...] = jnp.where(live, spot, 0)
    mine = live & (part == rank_me) & (rank < cap)
    position[...] = jnp.where(mine, offset * (CLASS_ROWS * 128) + rank, -1)
    local[...] = inside - rank_me * own_rows

    rows = patches * CLASS_ROWS

    def invert(i, total):
        at = pl.ds(i * 8, 8)
        spots = wide(position[at, :])
        edge = i * 1024 + iota((1, 1024), 1)
        line = wide(local[at, :])
        sender = wide(send_ref[at, :])
        here = iota((rows, 1024), 0) == (spots >> 7)
        values = [jnp.ones((1, 1024), jnp.int32)]
        for value in (line, edge, sender):
            values += [value >> 8, value & 255]
        left = jnp.concatenate(
            [jnp.where(here, value.astype(jnp.float32), 0.0).astype(jnp.bfloat16) for value in values], axis=0
        )
        right = one_hot(iota((128, 1024), 0) == (spots & 127))
        return total + dot_nt(left, right)

    total = lax.fori_loop(0, groups // 8, invert, jnp.zeros((7 * rows, 128), jnp.float32))
    filled = total[:rows] > 0.5

    def value_of(n):
        value = total[n * rows : (n + 1) * rows] * 256.0 + total[(n + 1) * rows : (n + 2) * rows]
        return jnp.where(filled, value, -1.0).astype(jnp.int32)

    last = (iota((rows, 128), 0) & (CLASS_ROWS - 1)) == CLASS_ROWS - 1
    req_ref[...] = jnp.where(last, over.astype(jnp.int32), value_of(1))
    edge_ref[...] = value_of(3)
    send_out_ref[...] = value_of(5)


def plan_edges(here, receivers, sender_local, mesh_slot, patches, ranks, mesh_rows):
    groups = receivers.shape[0] // 128
    mesh_total = mesh_slot.shape[0]
    high = mesh_total // 128
    parts = 1
    while 256**parts < mesh_total:
        parts += 1
    turned = mesh_slot.reshape(high, 128).T
    table = jnp.concatenate([((turned >> (8 * i)) & 255).astype(jnp.bfloat16) for i in range(parts)], 0)
    rows = patches * CLASS_ROWS
    vmem = pl.BlockSpec(memory_space=pltpu.VMEM)
    lists = jax.ShapeDtypeStruct((rows, 128), jnp.int32)
    return pl.pallas_call(
        functools.partial(index_kernel, (patches, ranks, mesh_rows, parts)),
        in_specs=[pl.BlockSpec(memory_space=pltpu.SMEM), vmem, vmem, vmem],
        out_specs=[vmem] * 4,
        out_shape=[lists, lists, lists, jax.ShapeDtypeStruct((groups, 128), jnp.int32)],
        scratch_shapes=[
            pltpu.VMEM((groups, 128), jnp.int32),
            pltpu.VMEM((patches * ranks * groups, 128), jnp.bfloat16),
            pltpu.VMEM((groups, 128), jnp.int32),
            pltpu.VMEM((groups, 128), jnp.int32),
            pltpu.VMEM((patches * ranks * groups, 256), jnp.float32),
        ],
        name="plan_edges",
    )(here, receivers.reshape(groups, 128), sender_local.reshape(groups, 128), table)


def stage_kernel(sizes, count, where, req, edges, sends, vector, w_edge, w_sender, w_receiver, w_edge_out, w_mesh_in, w_message_in, w_mesh_out, mesh, edge, grid, mesh_out, edge_out, flag, mesh_v, edge_v, grid_v, first_w, second_w, third_w, fourth_w, vectors, reqs, rows_out, rows_in, picked_e, picked_s, messages, outgoing, incoming, table, staged, finished, finished_mesh, local_sem, weight_send, weight_recv, req_send, req_recv, row_send, row_recv, msg_send, msg_recv, out_send, out_recv, mesh_send, mesh_recv, mesh_own):
    patches, ranks = sizes
    me, rank = lax.axis_index("patch"), lax.axis_index("hidden")
    starts, caps, chunks = class_plan(patches)
    far_first = OWN_CHUNKS + 2 * NEAR_CHUNKS
    full = first_w.shape[1]
    width = w_edge.shape[1]
    own_rows = mesh_v.shape[0]
    edge_rows = edge_v.shape[0]
    patch_peer = lambda k: lax.rem(me + k + patches, patches)
    rank_peer = lambda k: lax.rem(rank + k, ranks)
    own_columns = pl.ds(pl.multiple_of(rank * width, width), width)

    def class_of(chunk):
        near = (chunk - OWN_CHUNKS) // NEAR_CHUNKS
        is_near = (chunk >= OWN_CHUNKS) & (chunk < far_first)
        k = jnp.where(chunk < OWN_CHUNKS, 0, jnp.where(is_near, 1 + near * (patches - 2), chunk - far_first + 2))
        at = jnp.where(chunk < OWN_CHUNKS, chunk, jnp.where(is_near, (chunk - OWN_CHUNKS) % NEAR_CHUNKS, 0))
        return k, at

    def send(src, dst, send_sem, recv_sem, axis, peer):
        return pltpu.make_async_remote_copy(
            src_ref=src, dst_ref=dst, send_sem=send_sem, recv_sem=recv_sem,
            device_id={axis: peer}, device_id_type=pl.DeviceIdType.MESH,
        )

    weights = [
        (w_edge, first_w, 0, True),
        (w_sender, first_w, full, True),
        (w_receiver, first_w, 2 * full, True),
        (w_edge_out, second_w, 0, False),
        (w_mesh_in, third_w, 0, True),
        (w_message_in, third_w, full, True),
        (w_mesh_out, fourth_w, 0, False),
    ]

    def landing(entry):
        src, dst, first, by_column = entry
        if by_column:
            return dst.at[pl.ds(first, full), own_columns]
        return dst.at[own_columns, :]

    loads = [
        pltpu.make_async_copy(mesh.at[pl.ds(pl.multiple_of(rank * own_rows, 16), own_rows)], mesh_v, local_sem.at[0]),
        pltpu.make_async_copy(edge, edge_v, local_sem.at[1]),
        pltpu.make_async_copy(grid, grid_v, local_sem.at[2]),
        pltpu.make_async_copy(vector, vectors.at[rank], local_sem.at[3]),
    ]
    for n, entry in enumerate(weights):
        loads.append(pltpu.make_async_copy(entry[0], landing(entry), local_sem.at[4 + n]))
    for load in loads:
        load.start()

    gap = CHUNK - FAR_ROWS
    for chunk in range(far_first, chunks):
        messages[chunk, FAR_ROWS:, :] = jnp.zeros((gap, full), jnp.bfloat16)
    reqs[:CLASS_ROWS, :] = req[:CLASS_ROWS, :]

    barrier = pltpu.get_barrier_semaphore()
    for k in range(1, patches):
        pl.semaphore_signal(barrier, inc=1, device_id={"patch": patch_peer(k)}, device_id_type=pl.DeviceIdType.MESH)
    for k in range(1, ranks):
        pl.semaphore_signal(barrier, inc=1, device_id={"hidden": rank_peer(k)}, device_id_type=pl.DeviceIdType.MESH)
    pl.semaphore_wait(barrier, patches + ranks - 2)

    req_copies = []
    for k in range(1, patches):
        block = pl.ds(k * CLASS_ROWS, CLASS_ROWS)
        copy = send(req.at[block], reqs.at[block], req_send.at[k], req_recv.at[k], "patch", patch_peer(k))
        copy.start()
        req_copies.append(copy)
    weight_copies = []
    for k in range(1, ranks):
        copy = send(vector, vectors.at[rank], weight_send.at[k, 7], weight_recv.at[k, 7], "hidden", rank_peer(k))
        copy.start()
        weight_copies.append(copy)
        for n, entry in enumerate(weights):
            copy = send(entry[0], landing(entry), weight_send.at[k, n], weight_recv.at[k, n], "hidden", rank_peer(k))
            copy.start()
            weight_copies.append(copy)

    def columns(ref, k, at):
        turned = ref[pl.ds(pl.multiple_of(k * CLASS_ROWS, CLASS_ROWS), CLASS_ROWS), :].astype(jnp.float32).T
        lane = iota(turned.shape, 1)
        picks = [jnp.sum(jnp.where(lane == 2 * at + n, turned, 0.0), axis=1, keepdims=True) for n in range(2)]
        return jnp.concatenate(picks, axis=0).astype(jnp.int32)

    def pick(column, source, step):
        total = None
        for first in range(0, source.shape[0], step):
            hot = one_hot(iota((CHUNK, step), 1) == column - first)
            piece = dot(hot, source[first : first + step, :])
            total = piece if total is None else total + piece
        return total.astype(jnp.bfloat16)

    def rows_of(chunk, rows):
        return pl.ds(0, CHUNK if rows is None else rows)

    def row_copy(chunk, k, rows):
        part = pl.ds(0, rows)
        return send(
            rows_out.at[chunk, part], rows_in.at[chunk, part], row_send.at[chunk], row_recv.at[chunk], "patch", patch_peer(-k)
        )

    def msg_copy(chunk, k, rows):
        part = pl.ds(0, rows)
        return send(
            picked_s.at[chunk, part], messages.at[chunk, part], msg_send.at[chunk], msg_recv.at[chunk], "patch", patch_peer(k)
        )

    loads[0].wait()
    gather_step = own_rows if own_rows <= 1280 else CHUNK
    for copy in req_copies:
        copy.wait_recv()

    def serve(chunk, rows):
        k, at = class_of(chunk)
        rows_out[chunk] = pick(columns(reqs, k, at), mesh_v, gather_step)
        row_copy(chunk, k, rows).start()

    @pl.loop(far_first, chunks)
    def _(chunk):
        serve(chunk, FAR_ROWS)

    @pl.loop(OWN_CHUNKS, far_first)
    def _(chunk):
        serve(chunk, CHUNK)

    @pl.loop(0, OWN_CHUNKS)
    def _(chunk):
        rows_in[chunk] = pick(columns(reqs, 0, chunk), mesh_v, gather_step)

    loads[1].wait()
    loads[2].wait()

    @pl.loop(0, chunks)
    def _(chunk):
        k, at = class_of(chunk)
        picked_e[chunk] = pick(columns(edges, k, at), edge_v, 1024)
        picked_s[chunk] = pick(columns(sends, k, at), grid_v, 1024)

    for load in loads[3:]:
        load.wait()
    for copy in weight_copies:
        copy.wait_recv()

    def vector_row(n):
        return jnp.concatenate([vectors[j, n : n + 1, :] for j in range(ranks)], axis=1)

    def edge_mlp(chunk, rows):
        own_edge = picked_e[chunk, :rows, :]
        pre = dot(own_edge, first_w[:full, :])
        pre = pre + dot(picked_s[chunk, :rows, :], first_w[full : 2 * full, :])
        pre = pre + dot(rows_in[chunk, :rows, :], first_w[2 * full :, :]) + vector_row(0)
        hidden = jax.nn.silu(pre).astype(jnp.bfloat16)
        total = dot(hidden, second_w[...]) + vector_row(1)
        message = normalize(total, vector_row(2), vector_row(3))
        result = (own_edge.astype(jnp.float32) + message).astype(jnp.bfloat16)
        for j in range(ranks):
            outgoing[j, chunk, :rows, :] = result[:, j * width : (j + 1) * width]
        return message.astype(jnp.bfloat16)

    @pl.loop(0, OWN_CHUNKS)
    def _(chunk):
        messages[chunk] = edge_mlp(chunk, CHUNK)

    @pl.loop(OWN_CHUNKS, far_first)
    def _(chunk):
        k, _ = class_of(chunk)
        row_copy(chunk, k, CHUNK).wait_recv()
        picked_s[chunk] = edge_mlp(chunk, CHUNK)
        msg_copy(chunk, k, CHUNK).start()

    @pl.loop(far_first, chunks)
    def _(chunk):
        k, _ = class_of(chunk)
        row_copy(chunk, k, FAR_ROWS).wait_recv()
        picked_s[chunk, :FAR_ROWS, :] = edge_mlp(chunk, FAR_ROWS)
        msg_copy(chunk, k, FAR_ROWS).start()

    out_copies = []
    for k in range(1, ranks):
        peer = rank_peer(k)
        spans = [(pl.ds(0, far_first), pl.ds(0, CHUNK)), (pl.ds(far_first, chunks - far_first), pl.ds(0, FAR_ROWS))]
        for n, (block, part) in enumerate(spans):
            copy = send(
                outgoing.at[peer, block, part], incoming.at[rank, block, part],
                out_send.at[k, n], out_recv.at[k, n], "hidden", peer,
            )
            copy.start()
            out_copies.append(copy)

    @pl.loop(OWN_CHUNKS, far_first)
    def _(chunk):
        k, _ = class_of(chunk)
        msg_copy(chunk, k, CHUNK).wait_recv()

    @pl.loop(far_first, chunks)
    def _(chunk):
        k, _ = class_of(chunk)
        msg_copy(chunk, k, FAR_ROWS).wait_recv()

    plan = [(0, c) for c in range(OWN_CHUNKS)] + [(k, c) for k in (1, patches - 1) for c in range(NEAR_CHUNKS)]
    plan += [(k, 0) for k in range(2, patches - 1)]
    blocks = own_rows // CHUNK

    def mesh_copy(block, k):
        peer = rank_peer(k)
        at = pl.ds(pl.multiple_of(rank * own_rows + block * CHUNK, CHUNK), CHUNK)
        return send(
            finished_mesh.at[peer, pl.ds(pl.multiple_of(block * CHUNK, CHUNK), CHUNK)], mesh_out.at[at],
            mesh_send.at[k, block], mesh_recv.at[k, block], "hidden", peer,
        )

    def mesh_local(block):
        at = pl.ds(pl.multiple_of(rank * own_rows + block * CHUNK, CHUNK), CHUNK)
        return pltpu.make_async_copy(
            finished_mesh.at[rank, pl.ds(pl.multiple_of(block * CHUNK, CHUNK), CHUNK)], mesh_out.at[at], mesh_own.at[block]
        )

    @pl.loop(0, blocks)
    def _(block):
        at = pl.ds(pl.multiple_of(block * CHUNK, CHUNK), CHUNK)
        line = iota((CHUNK, CHUNK), 0) + block * CHUNK
        total = None
        for chunk, (k, c) in enumerate(plan):
            row = k * CLASS_ROWS + 2 * c
            wanted = jnp.concatenate([reqs[row : row + 1, :], reqs[row + 1 : row + 2, :]], axis=1)
            piece = dot(one_hot(line == wanted), messages[chunk])
            total = piece if total is None else total + piece
        own = mesh_v[at, :]
        pre = dot(own, third_w[:full, :]) + dot(total.astype(jnp.bfloat16), third_w[full:, :]) + vector_row(4)
        hidden = jax.nn.silu(pre).astype(jnp.bfloat16)
        total = dot(hidden, fourth_w[...]) + vector_row(5)
        update = normalize(total, vector_row(6), vector_row(7))
        result = (own.astype(jnp.float32) + update).astype(jnp.bfloat16)
        for j in range(ranks):
            finished_mesh[j, at, :] = result[:, j * width : (j + 1) * width]
        for k in range(1, ranks):
            mesh_copy(block, k).start()
        mesh_local(block).start()

    over = reqs[CLASS_ROWS - 1 : CLASS_ROWS, :]
    for k in range(1, patches):
        row = (k + 1) * CLASS_ROWS - 1
        over = jnp.maximum(over, reqs[row : row + 1, :])
    flag[...] = jnp.broadcast_to(over, flag.shape)

    for copy in out_copies:
        copy.wait_recv()

    @pl.loop(0, ranks)
    def _(j):
        @pl.when(j == rank)
        def _():
            @pl.loop(0, chunks)
            def _(chunk):
                table[pl.ds(pl.multiple_of((j * chunks + chunk) * CHUNK, CHUNK), CHUNK), :] = outgoing[j, chunk].astype(jnp.float32)

        @pl.when(j != rank)
        def _():
            @pl.loop(0, chunks)
            def _(chunk):
                table[pl.ds(pl.multiple_of((j * chunks + chunk) * CHUNK, CHUNK), CHUNK), :] = incoming[j, chunk].astype(jnp.float32)

    @pl.loop(0, edge_rows // CHUNK)
    def _(block):
        @pl.loop(0, CHUNK // 128)
        def _(line):
            @pl.loop(0, 128, step=16)
            def _(first):
                for n in range(16):
                    spot = where[block * (CHUNK // 128) + line, first + n]
                    staged[pl.ds(line * 128 + first + n, 1), :] = table[pl.ds(spot, 1), :]

        at = pl.ds(pl.multiple_of(block * CHUNK, CHUNK), CHUNK)
        live = iota((CHUNK, width), 0) + block * CHUNK < count[0]
        finished[at, :] = jnp.where(live, staged[...], edge_v[at, own_columns].astype(jnp.float32)).astype(jnp.bfloat16)

    last = pltpu.make_async_copy(finished, edge_out, local_sem.at[0])
    last.start()

    for copy in req_copies + weight_copies + out_copies:
        copy.wait_send()

    @pl.loop(OWN_CHUNKS, far_first)
    def _(chunk):
        k, _ = class_of(chunk)
        row_copy(chunk, k, CHUNK).wait_send()
        msg_copy(chunk, k, CHUNK).wait_send()

    @pl.loop(far_first, chunks)
    def _(chunk):
        k, _ = class_of(chunk)
        row_copy(chunk, k, FAR_ROWS).wait_send()
        msg_copy(chunk, k, FAR_ROWS).wait_send()

    @pl.loop(0, blocks)
    def _(block):
        for k in range(1, ranks):
            mesh_copy(block, k).wait()
        mesh_local(block).wait()

    last.wait()


def run_stages(patches, ranks, count, where, req, edges, sends, vector, weights, mesh_latent, edge_latent, grid_latent):
    full, width = weights[0].shape
    mesh_rows, edge_rows, grid_rows = mesh_latent.shape[0], edge_latent.shape[0], grid_latent.shape[0]
    own_rows = mesh_rows // ranks
    chunks = class_plan(patches)[2]
    bf16, f32 = jnp.bfloat16, jnp.float32
    dma = pltpu.SemaphoreType.DMA
    vmem = pl.BlockSpec(memory_space=pltpu.VMEM)
    smem = pl.BlockSpec(memory_space=pltpu.SMEM)
    hbm = pl.BlockSpec(memory_space=pl.ANY)
    blocks = own_rows // CHUNK
    return pl.pallas_call(
        functools.partial(stage_kernel, (patches, ranks)),
        in_specs=[smem, smem, vmem, vmem, vmem, vmem] + [hbm] * 10,
        out_specs=[hbm, hbm, vmem],
        out_shape=[
            jax.ShapeDtypeStruct((mesh_rows, width), bf16),
            jax.ShapeDtypeStruct((edge_rows, width), bf16),
            jax.ShapeDtypeStruct((8, 128), jnp.int32),
        ],
        scratch_shapes=[
            pltpu.VMEM((own_rows, full), bf16),
            pltpu.VMEM((edge_rows, full), bf16),
            pltpu.VMEM((grid_rows, full), bf16),
            pltpu.VMEM((3 * full, full), bf16),
            pltpu.VMEM((full, full), bf16),
            pltpu.VMEM((2 * full, full), bf16),
            pltpu.VMEM((full, full), bf16),
            pltpu.VMEM((ranks, 8, width), f32),
            pltpu.VMEM((patches * CLASS_ROWS, 128), jnp.int32),
            pltpu.VMEM((chunks, CHUNK, full), bf16),
            pltpu.VMEM((chunks, CHUNK, full), bf16),
            pltpu.VMEM((chunks, CHUNK, full), bf16),
            pltpu.VMEM((chunks, CHUNK, full), bf16),
            pltpu.VMEM((chunks, CHUNK, full), bf16),
            pltpu.VMEM((ranks, chunks, CHUNK, width), bf16),
            pltpu.VMEM((ranks, chunks, CHUNK, width), bf16),
            pltpu.VMEM((ranks * chunks * CHUNK, width), f32),
            pltpu.VMEM((CHUNK, width), f32),
            pltpu.VMEM((edge_rows, width), bf16),
            pltpu.VMEM((ranks, own_rows, width), bf16),
            dma((11,)),
            dma((ranks, 8)),
            dma((ranks, 8)),
            dma((patches,)),
            dma((patches,)),
            dma((chunks,)),
            dma((chunks,)),
            dma((chunks,)),
            dma((chunks,)),
            dma((ranks, 2)),
            dma((ranks, 2)),
            dma((ranks, blocks)),
            dma((ranks, blocks)),
            dma((blocks,)),
        ],
        compiler_params=pltpu.CompilerParams(
            collective_id=0, has_side_effects=True, vmem_limit_bytes=62 * 1024 * 1024
        ),
        name="run_stages",
    )(count, where, req, edges, sends, vector, *weights, mesh_latent, edge_latent, grid_latent)


def pieces(x, axis, size):
    return [x] + [lax.ppermute(x, axis, [((j + k) % size, j) for j in range(size)]) for k in range(1, size)]


def rows_at(x, index):
    return x.at[index].get(mode="promise_in_bounds")


def dense(patches, ranks, operands):
    (grid_latent, mesh_latent, edge_latent, senders, receivers, mesh_slot, edge_counts, w_edge, w_sender, w_receiver,
     edge_bias, w_edge_out, edge_out_bias, edge_gain, edge_shift, w_mesh_in, w_message_in, mesh_bias, w_mesh_out,
     mesh_out_bias, mesh_gain, mesh_shift) = operands
    me, rank = lax.axis_index("patch"), lax.axis_index("hidden")
    mesh_rows, edge_rows = mesh_latent.shape[0], edge_latent.shape[0]
    mesh_total = mesh_slot.shape[0]
    width = w_edge.shape[1]
    bf16 = jnp.bfloat16

    def own(x):
        return lax.dynamic_slice_in_dim(x, rank * width, width, 1)

    def turn(x, axis):
        full = jnp.concatenate(pieces(x, "hidden", ranks), axis)
        return full

    def natural(x):
        full = turn(x, 0)
        return jnp.roll(full, rank * width, 0)[None]

    def spread_mlp(pre, w_out, bias, gain, shift):
        hidden = turn(jax.nn.silu(pre).astype(bf16), 1)
        total = dot(hidden, turn(w_out, 0)) + natural(bias)
        center = jnp.mean(total, axis=1, keepdims=True)
        centered = total - center
        scale = lax.rsqrt(jnp.mean(centered * centered, axis=1, keepdims=True) + EPSILON)
        return own(centered * scale) * gain[None] + shift[None]

    table = jnp.concatenate(pieces(dot(mesh_latent, w_receiver).astype(bf16), "patch", patches), 0)
    target = lax.rem(rows_at(mesh_slot, receivers) + (mesh_total - me * mesh_rows), mesh_total)
    sent = rows_at(dot(grid_latent, w_sender), senders - me * grid_latent.shape[0])
    pre = dot(edge_latent, w_edge) + sent + rows_at(table, target).astype(jnp.float32) + edge_bias[None]
    message = spread_mlp(pre, w_edge_out, edge_out_bias, edge_gain, edge_shift)
    live = jnp.arange(edge_rows)[:, None] < edge_counts[0]
    message = jnp.where(live, message, 0.0)
    edge_out = (own(edge_latent).astype(jnp.float32) + message).astype(bf16)
    sums = jnp.zeros((mesh_total, width), jnp.float32).at[target].add(message, mode="promise_in_bounds")
    summed = sums[:mesh_rows]
    for k in range(1, patches):
        part = sums[k * mesh_rows : (k + 1) * mesh_rows].astype(bf16)
        part = lax.ppermute(part, "patch", [(j, (j + k) % patches) for j in range(patches)])
        summed = summed + part.astype(jnp.float32)
    summed = jnp.roll(turn(summed.astype(bf16), 1), rank * width, 1)
    pre = dot(mesh_latent, w_mesh_in) + dot(summed, w_message_in) + mesh_bias[None]
    update = spread_mlp(pre, w_mesh_out, mesh_out_bias, mesh_gain, mesh_shift)
    mesh_out = (own(mesh_latent).astype(jnp.float32) + update).astype(bf16)
    return mesh_out, edge_out


def shards(patches, ranks, *operands):
    (grid_latent, mesh_latent, edge_latent, senders, receivers, mesh_slot, edge_counts, w_edge, w_sender, w_receiver,
     edge_bias, w_edge_out, edge_out_bias, edge_gain, edge_shift, w_mesh_in, w_message_in, mesh_bias, w_mesh_out,
     mesh_out_bias, mesh_gain, mesh_shift) = operands
    mesh_rows, edge_rows, grid_rows = mesh_latent.shape[0], edge_latent.shape[0], grid_latent.shape[0]
    fits = (
        w_edge.shape[1] % 128 == 0
        and 4 < patches <= 16
        and edge_rows % 1024 == 0
        and grid_rows % 1024 == 0
        and mesh_rows % (ranks * CHUNK) == 0
        and mesh_slot.shape[0] % 1024 == 0
    )
    if not fits:
        return dense(patches, ranks, operands)
    me = lax.axis_index("patch").astype(jnp.int32)
    rank = lax.axis_index("hidden").astype(jnp.int32)
    here = jnp.stack([me, rank, edge_counts[0]])
    req, edges, sends, where = plan_edges(
        here, receivers, senders - me * grid_rows, mesh_slot, patches, ranks, mesh_rows
    )
    vector = jnp.stack(
        [edge_bias, edge_out_bias, edge_gain, edge_shift, mesh_bias, mesh_out_bias, mesh_gain, mesh_shift]
    )
    weights = (w_edge, w_sender, w_receiver, w_edge_out, w_mesh_in, w_message_in, w_mesh_out)
    mesh_out, edge_out, flag = run_stages(
        patches, ranks, edge_counts, where, req, edges, sends, vector, weights, mesh_latent, edge_latent, grid_latent
    )
    return lax.cond(
        flag[0, 0] > 0,
        lambda outs, args: dense(patches, ranks, args),
        lambda outs, args: outs,
        (mesh_out, edge_out),
        operands,
    )


def solution(mesh):
    columns, rows, line, patch = P(None, "hidden"), P("hidden", None), P("hidden"), P("patch", None)
    return jax.shard_map(
        functools.partial(shards, mesh.shape["patch"], mesh.shape["hidden"]),
        mesh=mesh,
        in_specs=(
            patch, patch, patch, P("patch"), P("patch"), P(), P("patch"),
            columns, columns, columns, line, rows, line, line, line,
            columns, columns, line, rows, line, line, line,
        ),
        out_specs=(P("patch", "hidden"), P("patch", "hidden")),
        check_vma=False,
    )
```

time: 460 us -> 165 us (0.36)
  the two profiles are of different devices: /device:TPU:1 before, /device:TPU:29 now
where the time goes in v1:
time: 165 us
  Pallas kernels  152 us (92%)
  local copies, waits for them, and re-layouts  6.95 us (4%)
  other arithmetic  3.69 us (2%)
  between operations  2.04 us (1%)
    pallas_call x1, Pallas kernels, run_stages(): pl.pallas_call(functools.partial(stage_kernel, (patches, ranks)), in_spec...  142 us
    pallas_call x1, Pallas kernels, plan_edges(): pl.pallas_call(functools.partial(index_kernel, (patches, ranks, mesh_rows...  9.5 us
    unnamed x14, local copies, waits for them, and re-layouts  4.13 us

profile of v1, /device:TPU:29, one launch (start us, length us, event | category | flops | bytes accessed | tf_op | source)
XLA Modules:
  0.0 164.7 jit_solution(9024309076268478724)
XLA Ops:
  1.3 0.7 pad_add_fusion.where_am_i
  1.9 1.0 fusion.55
  2.9 0.1 copy.51
  3.0 0.1 copy.50
  3.2 0.7 pad_maximum_fusion.table_ref
  3.9 1.4 subtract_bitcast_fusion.send_ref
  5.2 9.5 %plan_edges.1 = (s32[64,128]{1,0:T(8,128)}, s32[64,128]{1,0:T(8,128)}, s32[64,128]{1,0:T(8,128)}, s32[64,128]{1,0:T(8,128)}) custom-call(s32[3]{0:T(128)} %pad_add_fusion.where_am_i, s32[64,128]{1,0:T(8,128)} %bitcast.39, s32[64,128]{1,0:T(8,128)} %subtract_bitcast_fusion.send_ref, bf16[256,320]{1,0:T(8,128)(2,1)} %pad_maximum_fusion.table_ref), custom_call_target="tpu_custom_call" | custom-call | tf_op jit(solution)/shard_map/plan_edges/pallas_call | solution.py:159
  14.7 1.4 stack.47.vector
  16.1 0.0 copy-start
  16.1 0.0 copy-start.1
  16.1 0.0 copy-start.3
  16.1 0.0 copy-start.4
  16.1 0.0 copy-start.9
  16.1 142.3 %run_stages.1 = (bf16[5120,128]{1,0:T(8,128)(2,1)S(1)}, bf16[8192,128]{1,0:T(8,128)(2,1)}, s32[8,128]{1,0:T(8,128)}) custom-call(s32[1]{0:T(128)S(6)} %copy.84.count, s32[64,128]{1,0:T(8,128)} %get-tuple-element.80.where, s32[64,128]{1,0:T(8,128)} %get-tuple-element.81.req, s32[64,128]{1,0:T(8,128)} %get-tuple-element.82.edges, ...), custom_call_target="tpu_custom_call" | custom-call | tf_op jit(solution)/shard_map/run_stages/pallas_call | solution.py:492
  158.4 1.2 slice.34
  160.3 0.0 copy-done
  160.3 0.0 copy-done.1
  160.3 0.0 copy-done.2
  160.3 0.0 copy-done.3
  160.3 0.0 copy-done.4
  160.3 0.0 copy-done.9
  160.3 0.2 conditional.1
  160.5 1.1 copy.85
  161.6 3.0 %copy.86 = bf16[8192,128]{1,0:T(8,128)(2,1)} copy(bf16[8192,128]{1,0:T(8,128)(2,1)} %get-tuple-element.203) | data formatting | bytes 4194304
  (1 shorter events, 0.0 us)
Async XLA Ops:
  16.1 144.2 %copy-start = (s32[40960]{0:T(1024)S(1)}, s32[40960]{0:T(1024)}, u32[]{:S(2)}) copy-start(s32[40960]{0:T(1024)} %param.31) | copy-start | bytes 491524
  16.1 144.2 %copy-start.1 = (bf16[512,128]{1,0:T(8,128)(2,1)S(1)}, bf16[512,128]{1,0:T(8,128)(2,1)}, u32[]{:S(2)}) copy-start(bf16[512,128]{1,0:T(8,128)(2,1)} %w_edge.1) | copy-start | bytes 393220
  16.1 144.2 %copy-start.2 = (bf16[512,128]{1,0:T(8,128)(2,1)S(1)}, bf16[512,128]{1,0:T(8,128)(2,1)}, u32[]{:S(2)}) copy-start(bf16[512,128]{1,0:T(8,128)(2,1)} %w_sender.1) | copy-start | bytes 393220
  16.1 144.2 %copy-start.3 = (bf16[512,128]{1,0:T(8,128)(2,1)S(1)}, bf16[512,128]{1,0:T(8,128)(2,1)}, u32[]{:S(2)}) copy-start(bf16[512,128]{1,0:T(8,128)(2,1)} %w_receiver.1) | copy-start | bytes 393220
  16.1 144.2 %copy-start.4 = (bf16[512,128]{1,0:T(8,128)(2,1)S(1)}, bf16[512,128]{1,0:T(8,128)(2,1)}, u32[]{:S(2)}) copy-start(bf16[512,128]{1,0:T(8,128)(2,1)} %w_mesh_in.1) | copy-start | bytes 393220
  16.1 144.2 %copy-start.9 = (s32[8192]{0:T(1024)S(1)}, s32[8192]{0:T(1024)}, u32[]{:S(2)}) copy-start(s32[8192]{0:T(1024)} %param.29) | copy-start | bytes 98308

commit v2 on v1

v2 whole, which is shorter than its diff:
```python
import functools

import jax
import jax.numpy as jnp
from jax import lax
from jax.experimental import pallas as pl
from jax.experimental.pallas import tpu as pltpu
from jax.sharding import PartitionSpec as P

EPSILON = 1e-05
CHUNK = 256
OWN_CHUNKS = 3
NEAR_CHUNKS = 2
NEAR_ROWS = 240
FAR_ROWS = 176
CLASS_ROWS = 8


def iota(shape, axis):
    return lax.broadcasted_iota(jnp.int32, shape, axis)


def one_hot(cond):
    return jnp.where(cond, 1.0, 0.0).astype(jnp.bfloat16)


def dot(a, b):
    return jnp.dot(a, b, preferred_element_type=jnp.float32)


def dot_nt(a, b):
    return lax.dot_general(a, b, (((1,), (1,)), ((), ())), preferred_element_type=jnp.float32)


def within(index, size):
    if size & (size - 1) == 0:
        return index & (size - 1)
    return jnp.clip(index, 0, size - 1)


def wide(block):
    return jnp.concatenate([block[j : j + 1, :] for j in range(block.shape[0])], axis=1)


def normalize(total, gain, offset):
    width = total.shape[1]
    center = jnp.sum(total, axis=1, keepdims=True) / width
    centered = total - center
    spread = jnp.sum(centered * centered, axis=1, keepdims=True) / width
    return centered * lax.rsqrt(spread + EPSILON) * gain + offset


def class_plan(patches):
    starts = [0, OWN_CHUNKS] + [OWN_CHUNKS + 2 * NEAR_CHUNKS + k - 2 for k in range(2, patches - 1)]
    starts.append(OWN_CHUNKS + NEAR_CHUNKS)
    near = NEAR_CHUNKS * NEAR_ROWS
    caps = [OWN_CHUNKS * CHUNK, near] + [FAR_ROWS] * (patches - 3) + [near]
    return starts, caps, OWN_CHUNKS + 2 * NEAR_CHUNKS + patches - 3


def plan_edges(sizes, me, rank_me, count, recv_ref, send_ref, slot_ref, req_ref, edge_ref, send_out_ref, where_ref, slots, target, masks, position, local, totals):
    patches, ranks, mesh_rows, grid_rows, parts = sizes
    groups = recv_ref.shape[0]
    own_rows = mesh_rows // ranks
    starts, caps, chunks = class_plan(patches)
    high = slot_ref.shape[0]
    turned = slot_ref[...].astype(jnp.float32).T.astype(jnp.int32)
    for part in range(parts):
        slots[part * 128 : (part + 1) * 128, :] = ((turned >> (8 * part)) & 255).astype(jnp.float32).astype(jnp.bfloat16)

    def lookup(i, carry):
        row = wide(recv_ref[pl.ds(i * 8, 8), :])
        hot = one_hot(iota((high, 1024), 0) == (row >> 7))
        found = dot(slots[...], hot)
        low = iota((128, 1024), 0) == (row & 127)
        value = jnp.zeros((1, 1024), jnp.float32)
        for part in range(parts):
            piece = jnp.where(low, found[part * 128 : (part + 1) * 128], 0.0)
            value = value + float(256**part) * jnp.sum(piece, axis=0, keepdims=True)
        value = value.astype(jnp.int32)
        block = jnp.concatenate([value[:, j * 128 : (j + 1) * 128] for j in range(8)], axis=0)
        target[pl.ds(i * 8, 8), :] = block
        return carry

    lax.fori_loop(0, groups // 8, lookup, 0)

    shape = (groups, 128)
    goal = target[...]
    owner = sum((goal >= k * mesh_rows).astype(jnp.int32) for k in range(1, patches))
    inside = goal - owner * mesh_rows
    part = sum((inside >= k * own_rows).astype(jnp.int32) for k in range(1, ranks))
    offset = owner - me
    offset = jnp.where(offset < 0, offset + patches, offset)
    slot = iota(shape, 0) * 128 + iota(shape, 1)
    live = slot < count
    label = jnp.where(live, offset * ranks + part, -1)
    classes = patches * ranks
    for c in range(classes):
        masks[c * groups : (c + 1) * groups, :] = one_hot(label == c)
    steps = jnp.concatenate([one_hot(iota((128, 128), 0) <= iota((128, 128), 1)), jnp.ones((128, 128), jnp.bfloat16)], axis=1)
    totals[...] = dot(masks[...], steps)
    below = one_hot(iota((groups, groups), 1) < iota((groups, groups), 0))
    rank = jnp.zeros(shape, jnp.float32)
    over = jnp.zeros((1, 128), jnp.float32)
    for c in range(classes):
        block = totals[c * groups : (c + 1) * groups, :]
        inner, whole = block[:, :128], block[:, 128:]
        before = dot(below, whole.astype(jnp.bfloat16))
        mine = jnp.where(label == c, 1.0, 0.0)
        rank = rank + mine * (inner - 1.0 + before)
        full = before[groups - 1 :, :] + whole[groups - 1 :, :]
        over = jnp.maximum(over, jnp.where(full > float(caps[c // ranks]), 1.0, 0.0))
    rank = rank.astype(jnp.int32)
    first = jnp.zeros(shape, jnp.int32)
    cap = jnp.zeros(shape, jnp.int32)
    for k in range(patches):
        first = jnp.where(offset == k, starts[k] * CHUNK, first)
        cap = jnp.where(offset == k, caps[k], cap)
    fits = rank < cap
    near = (offset == 1) | (offset == patches - 1)
    rank = jnp.where(near & (rank >= NEAR_ROWS), rank + (CHUNK - NEAR_ROWS), rank)
    spot = part * (chunks * CHUNK) + first + rank
    spot = jnp.clip(spot, 0, ranks * chunks * CHUNK - 1)
    where_ref[...] = jnp.where(live, spot, 0)
    mine = live & (part == rank_me) & fits
    position[...] = jnp.where(mine, offset * (CLASS_ROWS * 128) + rank, -1)
    local[...] = inside - rank_me * own_rows

    rows = patches * CLASS_ROWS

    def invert(i, total):
        at = pl.ds(i * 8, 8)
        spots = wide(position[at, :])
        edge = i * 1024 + iota((1, 1024), 1)
        line = wide(local[at, :])
        sender = wide(send_ref[at, :]) - me * grid_rows
        here = iota((rows, 1024), 0) == (spots >> 7)
        values = [jnp.ones((1, 1024), jnp.int32)]
        for value in (line, edge, sender):
            values += [value >> 8, value & 255]
        left = jnp.concatenate(
            [jnp.where(here, value.astype(jnp.float32), 0.0).astype(jnp.bfloat16) for value in values], axis=0
        )
        right = one_hot(iota((128, 1024), 0) == (spots & 127))
        return total + dot_nt(left, right)

    total = lax.fori_loop(0, groups // 8, invert, jnp.zeros((7 * rows, 128), jnp.float32))
    filled = total[:rows] > 0.5

    def value_of(n, empty):
        value = total[n * rows : (n + 1) * rows] * 256.0 + total[(n + 1) * rows : (n + 2) * rows]
        return jnp.where(filled, value, empty).astype(jnp.int32)

    last = (iota((rows, 128), 0) & (CLASS_ROWS - 1)) == CLASS_ROWS - 1
    req_ref[...] = jnp.where(last, over.astype(jnp.int32), value_of(1, -1.0))
    edge_ref[...] = jnp.clip(value_of(3, 0.0), 0, groups * 128 - 1)
    send_out_ref[...] = value_of(5, 0.0)


def stage_kernel(sizes, count, receivers, senders, mesh_slot, bias_a, bias_b, gain_a, shift_a, bias_c, bias_d, gain_b, shift_b, w_edge, w_sender, w_receiver, w_edge_out, w_mesh_in, w_message_in, w_mesh_out, mesh, edge, grid, mesh_out, edge_out, flag, mesh_v, edge_v, grid_v, first_w, second_w, third_w, fourth_w, vectors, req, reqs, edges, sends, places, slots, target, masks, position, local, totals, edge_s, where, rows_out, rows_in, results, messages, outgoing, incoming, table, gathered, staged, finished, finished_mesh, local_sem, weight_send, weight_recv, req_send, req_recv, row_send, row_recv, msg_send, msg_recv, out_send, out_recv, mesh_send, mesh_recv, mesh_own):
    patches, ranks = sizes[0], sizes[1]
    me, rank = lax.axis_index("patch"), lax.axis_index("hidden")
    chunks = class_plan(patches)[2]
    far_first = OWN_CHUNKS + 2 * NEAR_CHUNKS
    full = first_w.shape[1]
    width = w_edge.shape[1]
    own_rows = mesh_v.shape[0]
    edge_rows = edge_v.shape[0]
    patch_peer = lambda k: lax.rem(me + k + patches, patches)
    rank_peer = lambda k: lax.rem(rank + k, ranks)
    side = rank + 1 - 2 * lax.rem(rank, 2)
    across = lax.rem(rank + 2, ranks)

    def class_of(chunk):
        near = (chunk - OWN_CHUNKS) // NEAR_CHUNKS
        is_near = (chunk >= OWN_CHUNKS) & (chunk < far_first)
        k = jnp.where(chunk < OWN_CHUNKS, 0, jnp.where(is_near, 1 + near * (patches - 2), chunk - far_first + 2))
        at = jnp.where(chunk < OWN_CHUNKS, chunk, jnp.where(is_near, (chunk - OWN_CHUNKS) % NEAR_CHUNKS, 0))
        return k, at

    def send(src, dst, send_sem, recv_sem, axis, peer):
        return pltpu.make_async_remote_copy(
            src_ref=src, dst_ref=dst, send_sem=send_sem, recv_sem=recv_sem,
            device_id={axis: peer}, device_id_type=pl.DeviceIdType.MESH,
        )

    weights = [
        (w_edge, first_w, 0, True),
        (w_sender, first_w, full, True),
        (w_receiver, first_w, 2 * full, True),
        (w_edge_out, second_w, 0, False),
        (w_mesh_in, third_w, 0, True),
        (w_message_in, third_w, full, True),
        (w_mesh_out, fourth_w, 0, False),
    ]
    edge_weights, mesh_weights = [7, 0, 1, 2, 3], [4, 5, 6]

    def landing(n, owner):
        if n == 7:
            return vectors.at[owner]
        _, dst, first, by_column = weights[n]
        columns = pl.ds(pl.multiple_of(owner * width, width), width)
        if by_column:
            return dst.at[pl.ds(first, full), columns]
        return dst.at[columns, :]

    def weight_copy(n, way):
        source = landing(n, across) if way == 2 else (vectors.at[rank] if n == 7 else weights[n][0])
        owner = across if way == 2 else rank
        peer = across if way == 1 else side
        return send(source, landing(n, owner), weight_send.at[way, n], weight_recv.at[way, n], "hidden", peer)

    loads = [
        pltpu.make_async_copy(mesh.at[pl.ds(pl.multiple_of(rank * own_rows, 16), own_rows)], mesh_v, local_sem.at[0]),
        pltpu.make_async_copy(edge, edge_v, local_sem.at[1]),
        pltpu.make_async_copy(grid, grid_v, local_sem.at[2]),
    ]
    for n, entry in enumerate(weights):
        loads.append(pltpu.make_async_copy(entry[0], landing(n, rank), local_sem.at[3 + n]))
    for load in loads:
        load.start()

    barrier = pltpu.get_barrier_semaphore()
    for k in range(1, patches):
        pl.semaphore_signal(barrier, inc=1, device_id={"patch": patch_peer(k)}, device_id_type=pl.DeviceIdType.MESH)
    for k in range(1, ranks):
        pl.semaphore_signal(barrier, inc=1, device_id={"hidden": rank_peer(k)}, device_id_type=pl.DeviceIdType.MESH)

    vectors[rank] = jnp.concatenate(
        [ref[...] for ref in (bias_a, bias_b, gain_a, shift_a, bias_c, bias_d, gain_b, shift_b)], axis=0
    )
    for chunk in range(OWN_CHUNKS, far_first):
        messages[chunk, NEAR_ROWS:, :] = jnp.zeros((CHUNK - NEAR_ROWS, full), jnp.bfloat16)
    for chunk in range(far_first, chunks):
        messages[chunk, FAR_ROWS:, :] = jnp.zeros((CHUNK - FAR_ROWS, full), jnp.bfloat16)

    pl.semaphore_wait(barrier, patches + ranks - 2)
    for n in edge_weights + mesh_weights:
        weight_copy(n, 1).start()
        weight_copy(n, 0).start()

    plan_edges(sizes, me, rank, count[0], receivers, senders, mesh_slot, req, edges, sends, places, slots, target, masks, position, local, totals)

    req_copies = []
    for k in range(1, patches):
        block = pl.ds(k * CLASS_ROWS, CLASS_ROWS)
        copy = send(req.at[block], reqs.at[block], req_send.at[k], req_recv.at[k], "patch", patch_peer(k))
        copy.start()
        req_copies.append(copy)
    reqs[:CLASS_ROWS, :] = req[:CLASS_ROWS, :]
    scalars = [
        pltpu.make_async_copy(edges, edge_s, local_sem.at[10]),
        pltpu.make_async_copy(places, where, local_sem.at[11]),
    ]
    for copy in scalars:
        copy.start()

    loads[1].wait()

    @pl.loop(0, edge_rows // CHUNK)
    def _(block):
        at = pl.multiple_of(block * CHUNK, CHUNK)
        for j in range(ranks):
            table[pl.ds(j * edge_rows + at, CHUNK), :] = edge_v[pl.ds(at, CHUNK), j * width : (j + 1) * width].astype(jnp.float32)

    def columns(ref, k, at):
        turned = ref[pl.ds(pl.multiple_of(k * CLASS_ROWS, CLASS_ROWS), CLASS_ROWS), :].astype(jnp.float32).T
        lane = iota(turned.shape, 1)
        picks = [jnp.sum(jnp.where(lane == 2 * at + n, turned, 0.0), axis=1, keepdims=True) for n in range(2)]
        return jnp.concatenate(picks, axis=0).astype(jnp.int32)

    def pick(column, source, step):
        total = None
        for first in range(0, source.shape[0], step):
            hot = one_hot(iota((column.shape[0], step), 1) == column - first)
            piece = dot(hot, source[first : first + step, :])
            total = piece if total is None else total + piece
        return total.astype(jnp.bfloat16)

    def row_copy(chunk, k, rows):
        part = pl.ds(0, rows)
        return send(
            rows_out.at[chunk, part], rows_in.at[chunk, part], row_send.at[chunk], row_recv.at[chunk], "patch", patch_peer(-k)
        )

    def msg_copy(chunk, k, rows):
        part = pl.ds(0, rows)
        return send(
            results.at[chunk, part], messages.at[chunk, part], msg_send.at[chunk], msg_recv.at[chunk], "patch", patch_peer(k)
        )

    def out_copy(chunk, k, rows):
        peer, part = rank_peer(k), pl.ds(0, rows)
        return send(
            outgoing.at[peer, chunk, part], incoming.at[rank, chunk, part],
            out_send.at[k, chunk], out_recv.at[k, chunk], "hidden", peer,
        )

    loads[0].wait()
    gather_step = own_rows if own_rows <= 1280 else CHUNK
    for copy in req_copies:
        copy.wait_recv()

    def serve(chunk, rows):
        k, at = class_of(chunk)
        rows_out[chunk] = pick(columns(reqs, k, at), mesh_v, gather_step)
        row_copy(chunk, k, rows).start()

    @pl.loop(far_first, chunks)
    def _(chunk):
        serve(chunk, FAR_ROWS)

    @pl.loop(OWN_CHUNKS, far_first)
    def _(chunk):
        serve(chunk, NEAR_ROWS)

    loads[2].wait()
    for copy in scalars:
        copy.wait()
    for load in loads[3:]:
        load.wait()
    for n in edge_weights:
        weight_copy(n, 1).wait_recv()
        weight_copy(n, 2).start()

    @pl.loop(0, OWN_CHUNKS)
    def _(chunk):
        rows_in[chunk] = pick(columns(reqs, 0, chunk), mesh_v, gather_step)

    for n in edge_weights:
        weight_copy(n, 0).wait_recv()
        weight_copy(n, 2).wait_recv()

    def vector_row(n):
        return jnp.concatenate([vectors[j, n : n + 1, :] for j in range(ranks)], axis=1)

    def collect(line, first, amount):
        for n in range(amount):
            spot = within(edge_s[line, n], edge_rows)
            for j in range(ranks):
                gathered[first + n : first + n + 1, j * width : (j + 1) * width] = table[pl.ds(j * edge_rows + spot, 1), :]

    def edge_stage(chunk, rows):
        k, at = class_of(chunk)
        collect(k * CLASS_ROWS + 2 * at, 0, 128)
        collect(k * CLASS_ROWS + 2 * at + 1, 128, rows - 128)
        own_edge = gathered[:rows, :]
        pre = dot(own_edge.astype(jnp.bfloat16), first_w[:full, :])
        sender = pick(columns(sends, k, at)[:rows], grid_v, 1024)
        pre = pre + dot(sender, first_w[full : 2 * full, :])
        return own_edge, pre

    def edge_finish(chunk, rows, own_edge, pre):
        pre = pre + dot(rows_in[chunk, :rows, :], first_w[2 * full :, :]) + vector_row(0)
        hidden = jax.nn.silu(pre).astype(jnp.bfloat16)
        total = dot(hidden, second_w[...]) + vector_row(1)
        message = normalize(total, vector_row(2), vector_row(3))
        result = (own_edge + message).astype(jnp.bfloat16)
        for j in range(ranks):
            outgoing[j, chunk, :rows, :] = result[:, j * width : (j + 1) * width]
        return message.astype(jnp.bfloat16)

    def remote_chunk(chunk, rows):
        k, _ = class_of(chunk)
        own_edge, pre = edge_stage(chunk, rows)
        row_copy(chunk, k, rows).wait_recv()
        results[chunk, :rows, :] = edge_finish(chunk, rows, own_edge, pre)
        msg_copy(chunk, k, rows).start()
        for j in range(1, ranks):
            out_copy(chunk, j, rows).start()

    @pl.loop(far_first, chunks)
    def _(chunk):
        remote_chunk(chunk, FAR_ROWS)

    @pl.loop(OWN_CHUNKS, far_first)
    def _(chunk):
        remote_chunk(chunk, NEAR_ROWS)

    @pl.loop(0, OWN_CHUNKS)
    def _(chunk):
        own_edge, pre = edge_stage(chunk, CHUNK)
        messages[chunk] = edge_finish(chunk, CHUNK, own_edge, pre)
        for j in range(1, ranks):
            out_copy(chunk, j, CHUNK).start()

    for n in mesh_weights:
        weight_copy(n, 1).wait_recv()
        weight_copy(n, 2).start()

    def each_chunk(act):
        @pl.loop(0, OWN_CHUNKS)
        def _(chunk):
            act(chunk, CHUNK, False)

        @pl.loop(OWN_CHUNKS, far_first)
        def _(chunk):
            act(chunk, NEAR_ROWS, True)

        @pl.loop(far_first, chunks)
        def _(chunk):
            act(chunk, FAR_ROWS, True)

    def await_out(chunk, rows, remote):
        for j in range(1, ranks):
            out_copy(chunk, j, rows).wait_recv()

    each_chunk(await_out)

    @pl.loop(0, ranks)
    def _(j):
        @pl.when(j == rank)
        def _():
            @pl.loop(0, chunks)
            def _(chunk):
                table[pl.ds(pl.multiple_of((j * chunks + chunk) * CHUNK, CHUNK), CHUNK), :] = outgoing[j, chunk].astype(jnp.float32)

        @pl.when(j != rank)
        def _():
            @pl.loop(0, chunks)
            def _(chunk):
                table[pl.ds(pl.multiple_of((j * chunks + chunk) * CHUNK, CHUNK), CHUNK), :] = incoming[j, chunk].astype(jnp.float32)

    own_columns = pl.ds(pl.multiple_of(rank * width, width), width)

    @pl.loop(0, edge_rows // 128)
    def _(line):
        for n in range(128):
            spot = within(where[line, n], table.shape[0])
            staged[n : n + 1, :] = table[pl.ds(spot, 1), :]
        at = pl.ds(pl.multiple_of(line * 128, 128), 128)
        live = iota((128, width), 0) + line * 128 < count[0]
        finished[at, :] = jnp.where(live, staged[...], edge_v[at, own_columns].astype(jnp.float32)).astype(jnp.bfloat16)

    last = pltpu.make_async_copy(finished, edge_out, local_sem.at[0])
    last.start()

    for n in mesh_weights:
        weight_copy(n, 0).wait_recv()
        weight_copy(n, 2).wait_recv()

    def await_msg(chunk, rows, remote):
        if remote:
            msg_copy(chunk, class_of(chunk)[0], rows).wait_recv()

    each_chunk(await_msg)

    plan = [(0, c) for c in range(OWN_CHUNKS)] + [(k, c) for k in (1, patches - 1) for c in range(NEAR_CHUNKS)]
    plan += [(k, 0) for k in range(2, patches - 1)]
    blocks = own_rows // CHUNK

    def mesh_copy(block, k):
        peer = rank_peer(k)
        at = pl.ds(pl.multiple_of(rank * own_rows + block * CHUNK, CHUNK), CHUNK)
        return send(
            finished_mesh.at[peer, pl.ds(pl.multiple_of(block * CHUNK, CHUNK), CHUNK)], mesh_out.at[at],
            mesh_send.at[k, block], mesh_recv.at[k, block], "hidden", peer,
        )

    def mesh_local(block):
        at = pl.ds(pl.multiple_of(rank * own_rows + block * CHUNK, CHUNK), CHUNK)
        return pltpu.make_async_copy(
            finished_mesh.at[rank, pl.ds(pl.multiple_of(block * CHUNK, CHUNK), CHUNK)], mesh_out.at[at], mesh_own.at[block]
        )

    @pl.loop(0, blocks)
    def _(block):
        at = pl.ds(pl.multiple_of(block * CHUNK, CHUNK), CHUNK)
        line = iota((CHUNK, CHUNK), 0) + block * CHUNK
        total = None
        for chunk, (k, c) in enumerate(plan):
            row = k * CLASS_ROWS + 2 * c
            wanted = jnp.concatenate([reqs[row : row + 1, :], reqs[row + 1 : row + 2, :]], axis=1)
            piece = dot(one_hot(line == wanted), messages[chunk])
            total = piece if total is None else total + piece
        own = mesh_v[at, :]
        pre = dot(own, third_w[:full, :]) + dot(total.astype(jnp.bfloat16), third_w[full:, :]) + vector_row(4)
        hidden = jax.nn.silu(pre).astype(jnp.bfloat16)
        total = dot(hidden, fourth_w[...]) + vector_row(5)
        update = normalize(total, vector_row(6), vector_row(7))
        result = (own.astype(jnp.float32) + update).astype(jnp.bfloat16)
        for j in range(ranks):
            finished_mesh[j, at, :] = result[:, j * width : (j + 1) * width]
        for k in range(1, ranks):
            mesh_copy(block, k).start()
        mesh_local(block).start()

    over = reqs[CLASS_ROWS - 1 : CLASS_ROWS, :]
    for k in range(1, patches):
        row = (k + 1) * CLASS_ROWS - 1
        over = jnp.maximum(over, reqs[row : row + 1, :])
    flag[...] = jnp.broadcast_to(over, flag.shape)

    for copy in req_copies:
        copy.wait_send()
    for way in range(3):
        for n in edge_weights + mesh_weights:
            weight_copy(n, way).wait_send()

    def drain(chunk, rows, remote):
        for j in range(1, ranks):
            out_copy(chunk, j, rows).wait_send()
        if remote:
            k = class_of(chunk)[0]
            row_copy(chunk, k, rows).wait_send()
            msg_copy(chunk, k, rows).wait_send()

    each_chunk(drain)

    @pl.loop(0, blocks)
    def _(block):
        for k in range(1, ranks):
            mesh_copy(block, k).wait()
        mesh_local(block).wait()

    last.wait()


def run_stages(patches, ranks, count, receivers, senders, mesh_slot, vectors, weights, mesh_latent, edge_latent, grid_latent):
    full, width = weights[0].shape
    mesh_rows, edge_rows, grid_rows = mesh_latent.shape[0], edge_latent.shape[0], grid_latent.shape[0]
    own_rows = mesh_rows // ranks
    chunks = class_plan(patches)[2]
    groups, high = edge_rows // 128, mesh_slot.shape[0] // 128
    parts = 1
    while 256**parts < mesh_slot.shape[0]:
        parts += 1
    bf16, f32, i32 = jnp.bfloat16, jnp.float32, jnp.int32
    dma = pltpu.SemaphoreType.DMA
    vmem = pl.BlockSpec(memory_space=pltpu.VMEM)
    smem = pl.BlockSpec(memory_space=pltpu.SMEM)
    hbm = pl.BlockSpec(memory_space=pl.ANY)
    blocks = own_rows // CHUNK
    lists = patches * CLASS_ROWS
    classes = patches * ranks * groups
    return pl.pallas_call(
        functools.partial(stage_kernel, (patches, ranks, mesh_rows, grid_rows, parts)),
        in_specs=[smem] + [vmem] * 11 + [hbm] * 10,
        out_specs=[hbm, hbm, vmem],
        out_shape=[
            jax.ShapeDtypeStruct((mesh_rows, width), bf16),
            jax.ShapeDtypeStruct((edge_rows, width), bf16),
            jax.ShapeDtypeStruct((8, 128), i32),
        ],
        scratch_shapes=[
            pltpu.VMEM((own_rows, full), bf16),
            pltpu.VMEM((edge_rows, full), bf16),
            pltpu.VMEM((grid_rows, full), bf16),
            pltpu.VMEM((3 * full, full), bf16),
            pltpu.VMEM((full, full), bf16),
            pltpu.VMEM((2 * full, full), bf16),
            pltpu.VMEM((full, full), bf16),
            pltpu.VMEM((ranks, 8, width), f32),
            pltpu.VMEM((lists, 128), i32),
            pltpu.VMEM((lists, 128), i32),
            pltpu.VMEM((lists, 128), i32),
            pltpu.VMEM((lists, 128), i32),
            pltpu.VMEM((groups, 128), i32),
            pltpu.VMEM((parts * 128, high), bf16),
            pltpu.VMEM((groups, 128), i32),
            pltpu.VMEM((classes, 128), bf16),
            pltpu.VMEM((groups, 128), i32),
            pltpu.VMEM((groups, 128), i32),
            pltpu.VMEM((classes, 256), f32),
            pltpu.SMEM((lists, 128), i32),
            pltpu.SMEM((groups, 128), i32),
            pltpu.VMEM((chunks, CHUNK, full), bf16),
            pltpu.VMEM((chunks, CHUNK, full), bf16),
            pltpu.VMEM((chunks, CHUNK, full), bf16),
            pltpu.VMEM((chunks, CHUNK, full), bf16),
            pltpu.VMEM((ranks, chunks, CHUNK, width), bf16),
            pltpu.VMEM((ranks, chunks, CHUNK, width), bf16),
            pltpu.VMEM((ranks * max(edge_rows, chunks * CHUNK), width), f32),
            pltpu.VMEM((CHUNK, full), f32),
            pltpu.VMEM((128, width), f32),
            pltpu.VMEM((edge_rows, width), bf16),
            pltpu.VMEM((ranks, own_rows, width), bf16),
            dma((12,)),
            dma((3, 8)),
            dma((3, 8)),
            dma((patches,)),
            dma((patches,)),
            dma((chunks,)),
            dma((chunks,)),
            dma((chunks,)),
            dma((chunks,)),
            dma((ranks, chunks)),
            dma((ranks, chunks)),
            dma((ranks, blocks)),
            dma((ranks, blocks)),
            dma((blocks,)),
        ],
        compiler_params=pltpu.CompilerParams(
            collective_id=0, has_side_effects=True, vmem_limit_bytes=67043328
        ),
        name="run_stages",
    )(
        count, receivers.reshape(groups, 128), senders.reshape(groups, 128), mesh_slot.reshape(high, 128),
        *[vector[None] for vector in vectors], *weights, mesh_latent, edge_latent, grid_latent,
    )


def pieces(x, axis, size):
    return [x] + [lax.ppermute(x, axis, [((j + k) % size, j) for j in range(size)]) for k in range(1, size)]


def rows_at(x, index):
    return x.at[index].get(mode="promise_in_bounds")


def dense(patches, ranks, operands):
    (grid_latent, mesh_latent, edge_latent, senders, receivers, mesh_slot, edge_counts, w_edge, w_sender, w_receiver,
     edge_bias, w_edge_out, edge_out_bias, edge_gain, edge_shift, w_mesh_in, w_message_in, mesh_bias, w_mesh_out,
     mesh_out_bias, mesh_gain, mesh_shift) = operands
    me, rank = lax.axis_index("patch"), lax.axis_index("hidden")
    mesh_rows, edge_rows = mesh_latent.shape[0], edge_latent.shape[0]
    mesh_total = mesh_slot.shape[0]
    width = w_edge.shape[1]
    bf16 = jnp.bfloat16

    def own(x):
        return lax.dynamic_slice_in_dim(x, rank * width, width, 1)

    def turn(x, axis):
        full = jnp.concatenate(pieces(x, "hidden", ranks), axis)
        return full

    def natural(x):
        full = turn(x, 0)
        return jnp.roll(full, rank * width, 0)[None]

    def spread_mlp(pre, w_out, bias, gain, shift):
        w_full, bias_full = turn(w_out, 0), natural(bias)
        step = CHUNK if pre.shape[0] % CHUNK == 0 else pre.shape[0]

        def block(i, result):
            part = lax.dynamic_slice_in_dim(pre, i * step, step, 0)
            hidden = turn(jax.nn.silu(part).astype(bf16), 1)
            total = dot(hidden, w_full) + bias_full
            center = jnp.mean(total, axis=1, keepdims=True)
            centered = total - center
            scale = lax.rsqrt(jnp.mean(centered * centered, axis=1, keepdims=True) + EPSILON)
            update = own(centered * scale) * gain[None] + shift[None]
            return lax.dynamic_update_slice_in_dim(result, update, i * step, 0)

        return lax.fori_loop(0, pre.shape[0] // step, block, jnp.zeros(pre.shape, jnp.float32))

    table = jnp.concatenate(pieces(dot(mesh_latent, w_receiver).astype(bf16), "patch", patches), 0)
    target = lax.rem(rows_at(mesh_slot, receivers) + (mesh_total - me * mesh_rows), mesh_total)
    sent = rows_at(dot(grid_latent, w_sender), senders - me * grid_latent.shape[0])
    pre = dot(edge_latent, w_edge) + sent + rows_at(table, target).astype(jnp.float32) + edge_bias[None]
    message = spread_mlp(pre, w_edge_out, edge_out_bias, edge_gain, edge_shift)
    live = jnp.arange(edge_rows)[:, None] < edge_counts[0]
    message = jnp.where(live, message, 0.0)
    edge_out = (own(edge_latent).astype(jnp.float32) + message).astype(bf16)
    rounded = message.astype(bf16)

    def add_block(i, sums):
        hot = (target[None] == (i * CHUNK + jnp.arange(CHUNK))[:, None]).astype(bf16)
        return lax.dynamic_update_slice_in_dim(sums, dot(hot, rounded), i * CHUNK, 0)

    sums = jnp.zeros((mesh_total, width), jnp.float32)
    if mesh_total % CHUNK:
        sums = sums.at[target].add(message, mode="promise_in_bounds")
    else:
        sums = lax.fori_loop(0, mesh_total // CHUNK, add_block, sums)
    summed = sums[:mesh_rows]
    for k in range(1, patches):
        part = sums[k * mesh_rows : (k + 1) * mesh_rows].astype(bf16)
        part = lax.ppermute(part, "patch", [(j, (j + k) % patches) for j in range(patches)])
        summed = summed + part.astype(jnp.float32)
    summed = jnp.roll(turn(summed.astype(bf16), 1), rank * width, 1)
    pre = dot(mesh_latent, w_mesh_in) + dot(summed, w_message_in) + mesh_bias[None]
    update = spread_mlp(pre, w_mesh_out, mesh_out_bias, mesh_gain, mesh_shift)
    mesh_out = (own(mesh_latent).astype(jnp.float32) + update).astype(bf16)
    return mesh_out, edge_out


def shards(patches, ranks, *operands):
    (grid_latent, mesh_latent, edge_latent, senders, receivers, mesh_slot, edge_counts, w_edge, w_sender, w_receiver,
     edge_bias, w_edge_out, edge_out_bias, edge_gain, edge_shift, w_mesh_in, w_message_in, mesh_bias, w_mesh_out,
     mesh_out_bias, mesh_gain, mesh_shift) = operands
    mesh_rows, edge_rows, grid_rows = mesh_latent.shape[0], edge_latent.shape[0], grid_latent.shape[0]
    fits = (
        w_edge.shape[1] % 128 == 0
        and ranks == 4
        and 4 < patches <= 16
        and edge_rows % 1024 == 0
        and grid_rows % 1024 == 0
        and mesh_rows % (ranks * CHUNK) == 0
        and mesh_slot.shape[0] % 1024 == 0
    )
    if not fits:
        return dense(patches, ranks, operands)
    vectors = (edge_bias, edge_out_bias, edge_gain, edge_shift, mesh_bias, mesh_out_bias, mesh_gain, mesh_shift)
    weights = (w_edge, w_sender, w_receiver, w_edge_out, w_mesh_in, w_message_in, w_mesh_out)
    mesh_out, edge_out, flag = run_stages(
        patches, ranks, edge_counts, receivers, senders, mesh_slot, vectors, weights, mesh_latent, edge_latent, grid_latent
    )
    return lax.cond(
        flag[0, 0] > 0,
        lambda outs, args: dense(patches, ranks, args),
        lambda outs, args: outs,
        (mesh_out, edge_out),
        operands,
    )


def solution(mesh):
    columns, rows, line, patch = P(None, "hidden"), P("hidden", None), P("hidden"), P("patch", None)
    return jax.shard_map(
        functools.partial(shards, mesh.shape["patch"], mesh.shape["hidden"]),
        mesh=mesh,
        in_specs=(
            patch, patch, patch, P("patch"), P("patch"), P(), P("patch"),
            columns, columns, columns, line, rows, line, line, line,
            columns, columns, line, rows, line, line, line,
        ),
        out_specs=(P("patch", "hidden"), P("patch", "hidden")),
        check_vma=False,
    )
```

time: 165 us -> 147 us (0.89)
  the two profiles are of different devices: /device:TPU:29 before, /device:TPU:1 now
where the time goes in v2:
time: 147 us; the launch traced here: 146 us
  Pallas kernels  139 us (95%)
  local copies, waits for them, and re-layouts  5.13 us (3%)
  between operations  1.95 us (1%)
    pallas_call x1, Pallas kernels, run_stages(): pl.pallas_call(functools.partial(stage_kernel, (patches, ranks, mesh_rows...  139 us
    unnamed x4, local copies, waits for them, and re-layouts  3.93 us

profile of v2, /device:TPU:1, one launch (start us, length us, event | category | flops | bytes accessed | tf_op | source)
XLA Modules:
  0.0 146.3 jit_solution(2219167083892775785)
XLA Ops:
  1.3 139.0 %run_stages.1 = (bf16[5120,128]{1,0:T(8,128)(2,1)}, bf16[8192,128]{1,0:T(8,128)(2,1)}, s32[8,128]{1,0:T(8,128)}) custom-call(s32[1]{0:T(128)S(6)} %copy.69.count, s32[64,128]{1,0:T(8,128)} %bitcast.42, s32[64,128]{1,0:T(8,128)} %bitcast.43, s32[320,128]{1,0:T(8,128)} %bitcast.41, f32[1,128]{1,0:T(1,128)} %bitcast.57, f32[1,128]{1,0:T(1,128)} %bitcast.51, ...), custom_call_target="tpu_custom_call" | custom-call | tf_op jit(solution)/shard_map/run_stages/pallas_call | solution.py:536
  140.3 1.2 slice.34
  142.2 0.2 conditional.1
  142.4 0.0 copy-start.2
  142.4 2.6 %copy.70 = bf16[5120,128]{1,0:T(8,128)(2,1)} copy(bf16[5120,128]{1,0:T(8,128)(2,1)} %get-tuple-element.852) | data formatting | bytes 2621440
  145.0 0.0 copy-done.2
  145.0 1.3 copy.71
Async XLA Ops:
  142.4 2.6 %copy-start.2 = (bf16[8192,128]{1,0:T(8,128)(2,1)S(1)}, bf16[8192,128]{1,0:T(8,128)(2,1)}, u32[]{:S(2)}) copy-start(bf16[8192,128]{1,0:T(8,128)(2,1)} %get-tuple-element.853) | copy-start | bytes 6291460

commit v3 on v2

--- a/solution.py
+++ b/solution.py
@@ -82,7 +82,7 @@
         target[pl.ds(i * 8, 8), :] = block
         return carry
 
-    lax.fori_loop(0, groups // 8, lookup, 0)
+    lax.fori_loop(0, groups // 8, lookup, 0, unroll=2)
 
     shape = (groups, 128)
     goal = target[...]
@@ -128,36 +128,37 @@
 
     rows = patches * CLASS_ROWS
 
-    def invert(i, total):
-        at = pl.ds(i * 8, 8)
-        spots = wide(position[at, :])
-        edge = i * 1024 + iota((1, 1024), 1)
-        line = wide(local[at, :])
-        sender = wide(send_ref[at, :]) - me * grid_rows
-        here = iota((rows, 1024), 0) == (spots >> 7)
-        values = [jnp.ones((1, 1024), jnp.int32)]
-        for value in (line, edge, sender):
-            values += [value >> 8, value & 255]
-        left = jnp.concatenate(
-            [jnp.where(here, value.astype(jnp.float32), 0.0).astype(jnp.bfloat16) for value in values], axis=0
+    def invert(read, amount):
+        def step(i, total):
+            at = pl.ds(i * 8, 8)
+            spots = wide(position[at, :])
+            here = iota((rows, 1024), 0) == (spots >> 7)
+            values = [part for value in read(i, at) for part in (value >> 8, value & 255)]
+            left = jnp.concatenate(
+                [jnp.where(here, value.astype(jnp.float32), 0.0).astype(jnp.bfloat16) for value in values], axis=0
+            )
+            right = one_hot(iota((128, 1024), 0) == (spots & 127))
+            return total + dot_nt(left, right)
+
+        total = lax.fori_loop(0, groups // 8, step, jnp.zeros((2 * amount * rows, 128), jnp.float32))
+        pairs = [total[n * rows : (n + 1) * rows] for n in range(2 * amount)]
+        return [(pairs[2 * n] * 256.0 + pairs[2 * n + 1]).astype(jnp.int32) for n in range(amount)]
+
+    last = (iota((rows, 128), 0) & (CLASS_ROWS - 1)) == CLASS_ROWS - 1
+    asked = invert(lambda i, at: [wide(local[at, :]) + 1], 1)[0] - 1
+    req_ref[...] = jnp.where(last, over.astype(jnp.int32), asked)
+
+    def finish():
+        edge, sender = invert(
+            lambda i, at: [i * 1024 + iota((1, 1024), 1), wide(send_ref[at, :]) - me * grid_rows], 2
         )
-        right = one_hot(iota((128, 1024), 0) == (spots & 127))
-        return total + dot_nt(left, right)
-
-    total = lax.fori_loop(0, groups // 8, invert, jnp.zeros((7 * rows, 128), jnp.float32))
-    filled = total[:rows] > 0.5
-
-    def value_of(n, empty):
-        value = total[n * rows : (n + 1) * rows] * 256.0 + total[(n + 1) * rows : (n + 2) * rows]
-        return jnp.where(filled, value, empty).astype(jnp.int32)
-
-    last = (iota((rows, 128), 0) & (CLASS_ROWS - 1)) == CLASS_ROWS - 1
-    req_ref[...] = jnp.where(last, over.astype(jnp.int32), value_of(1, -1.0))
-    edge_ref[...] = jnp.clip(value_of(3, 0.0), 0, groups * 128 - 1)
-    send_out_ref[...] = value_of(5, 0.0)
-
-
-def stage_kernel(sizes, count, receivers, senders, mesh_slot, bias_a, bias_b, gain_a, shift_a, bias_c, bias_d, gain_b, shift_b, w_edge, w_sender, w_receiver, w_edge_out, w_mesh_in, w_message_in, w_mesh_out, mesh, edge, grid, mesh_out, edge_out, flag, mesh_v, edge_v, grid_v, first_w, second_w, third_w, fourth_w, vectors, req, reqs, edges, sends, places, slots, target, masks, position, local, totals, edge_s, where, rows_out, rows_in, results, messages, outgoing, incoming, table, gathered, staged, finished, finished_mesh, local_sem, weight_send, weight_recv, req_send, req_recv, row_send, row_recv, msg_send, msg_recv, out_send, out_recv, mesh_send, mesh_recv, mesh_own):
+        edge_ref[...] = jnp.clip(edge, 0, groups * 128 - 1)
+        send_out_ref[...] = sender
+
+    return finish
+
+
+def stage_kernel(sizes, count, receivers, senders, mesh_slot, bias_a, bias_b, gain_a, shift_a, bias_c, bias_d, gain_b, shift_b, w_edge, w_sender, w_receiver, w_edge_out, w_mesh_in, w_message_in, w_mesh_out, mesh, edge, grid, mesh_out, edge_out, flag, mesh_v, edge_v, grid_v, first_w, second_w, third_w, fourth_w, vectors, req, reqs, edges, sends, places, slots, target, masks, position, local, totals, edge_s, where, rows_out, rows_in, results, messages, outgoing, incoming, table, gathered, staged, finished, finished_mesh, summed, local_sem, weight_send, weight_recv, req_send, req_recv, row_send, row_recv, msg_send, msg_recv, out_send, out_recv, mesh_send, mesh_recv, mesh_own):
     patches, ranks = sizes[0], sizes[1]
     me, rank = lax.axis_index("patch"), lax.axis_index("hidden")
     chunks = class_plan(patches)[2]
@@ -239,7 +240,7 @@
         weight_copy(n, 1).start()
         weight_copy(n, 0).start()
 
-    plan_edges(sizes, me, rank, count[0], receivers, senders, mesh_slot, req, edges, sends, places, slots, target, masks, position, local, totals)
+    finish_plan = plan_edges(sizes, me, rank, count[0], receivers, senders, mesh_slot, req, edges, sends, places, slots, target, masks, position, local, totals)
 
     req_copies = []
     for k in range(1, patches):
@@ -248,6 +249,7 @@
         copy.start()
         req_copies.append(copy)
     reqs[:CLASS_ROWS, :] = req[:CLASS_ROWS, :]
+    finish_plan()
     scalars = [
         pltpu.make_async_copy(edges, edge_s, local_sem.at[10]),
         pltpu.make_async_copy(places, where, local_sem.at[11]),
@@ -303,16 +305,23 @@
 
     def serve(chunk, rows):
         k, at = class_of(chunk)
-        rows_out[chunk] = pick(columns(reqs, k, at), mesh_v, gather_step)
+        rows_out[chunk, :rows, :] = pick(columns(reqs, k, at)[:rows], mesh_v, gather_step)
         row_copy(chunk, k, rows).start()
 
-    @pl.loop(far_first, chunks)
-    def _(chunk):
-        serve(chunk, FAR_ROWS)
-
-    @pl.loop(OWN_CHUNKS, far_first)
-    def _(chunk):
-        serve(chunk, NEAR_ROWS)
+    far_count, near_count = chunks - far_first, far_first - OWN_CHUNKS
+
+    def in_turn(act):
+        @pl.loop(0, max(far_count, near_count))
+        def _(j):
+            @pl.when(j < far_count)
+            def _():
+                act(far_first + j, FAR_ROWS)
+
+            @pl.when(j < near_count)
+            def _():
+                act(OWN_CHUNKS + j, NEAR_ROWS)
+
+    in_turn(serve)
 
     loads[2].wait()
     for copy in scalars:
@@ -338,13 +347,18 @@
         for n in range(amount):
             spot = within(edge_s[line, n], edge_rows)
             for j in range(ranks):
-                gathered[first + n : first + n + 1, j * width : (j + 1) * width] = table[pl.ds(j * edge_rows + spot, 1), :]
+                gathered[j, pl.ds(first + n, 1), :] = table[pl.ds(j * edge_rows + spot, 1), :]
 
     def edge_stage(chunk, rows):
         k, at = class_of(chunk)
-        collect(k * CLASS_ROWS + 2 * at, 0, 128)
-        collect(k * CLASS_ROWS + 2 * at + 1, 128, rows - 128)
-        own_edge = gathered[:rows, :]
+        if rows == CHUNK:
+            @pl.loop(0, 2)
+            def _(half):
+                collect(k * CLASS_ROWS + 2 * at + half, pl.multiple_of(half * 128, 128), 128)
+        else:
+            collect(k * CLASS_ROWS + 2 * at, 0, 128)
+            collect(k * CLASS_ROWS + 2 * at + 1, 128, rows - 128)
+        own_edge = jnp.concatenate([gathered[j, :rows, :] for j in range(ranks)], axis=1)
         pre = dot(own_edge.astype(jnp.bfloat16), first_w[:full, :])
         sender = pick(columns(sends, k, at)[:rows], grid_v, 1024)
         pre = pre + dot(sender, first_w[full : 2 * full, :])
@@ -369,14 +383,6 @@
         for j in range(1, ranks):
             out_copy(chunk, j, rows).start()
 
-    @pl.loop(far_first, chunks)
-    def _(chunk):
-        remote_chunk(chunk, FAR_ROWS)
-
-    @pl.loop(OWN_CHUNKS, far_first)
-    def _(chunk):
-        remote_chunk(chunk, NEAR_ROWS)
-
     @pl.loop(0, OWN_CHUNKS)
     def _(chunk):
         own_edge, pre = edge_stage(chunk, CHUNK)
@@ -384,6 +390,8 @@
         for j in range(1, ranks):
             out_copy(chunk, j, CHUNK).start()
 
+    in_turn(remote_chunk)
+
     for n in mesh_weights:
         weight_copy(n, 1).wait_recv()
         weight_copy(n, 2).start()
@@ -404,6 +412,29 @@
     def await_out(chunk, rows, remote):
         for j in range(1, ranks):
             out_copy(chunk, j, rows).wait_recv()
+
+    blocks = own_rows // CHUNK
+
+    def await_message(chunk, rows):
+        msg_copy(chunk, class_of(chunk)[0], rows).wait_recv()
+
+    def add_messages(chunk):
+        k, at = class_of(chunk)
+        row = pl.multiple_of(k * CLASS_ROWS, CLASS_ROWS)
+        asked = reqs[pl.ds(row, CLASS_ROWS), :]
+        line = iota(asked.shape, 0)
+        pair = [jnp.sum(jnp.where(line == 2 * at + n, asked, 0), axis=0, keepdims=True) for n in range(2)]
+        wanted = jnp.concatenate(pair, axis=1)
+        for block in range(blocks):
+            span = slice(block * CHUNK, (block + 1) * CHUNK)
+            hot = one_hot(iota((CHUNK, CHUNK), 0) + block * CHUNK == wanted)
+            summed[span, :] += dot(hot, messages[chunk])
+
+    summed[...] = jnp.zeros(summed.shape, jnp.float32)
+
+    @pl.loop(0, OWN_CHUNKS)
+    def _(chunk):
+        add_messages(chunk)
 
     each_chunk(await_out)
 
@@ -439,16 +470,6 @@
         weight_copy(n, 0).wait_recv()
         weight_copy(n, 2).wait_recv()
 
-    def await_msg(chunk, rows, remote):
-        if remote:
-            msg_copy(chunk, class_of(chunk)[0], rows).wait_recv()
-
-    each_chunk(await_msg)
-
-    plan = [(0, c) for c in range(OWN_CHUNKS)] + [(k, c) for k in (1, patches - 1) for c in range(NEAR_CHUNKS)]
-    plan += [(k, 0) for k in range(2, patches - 1)]
-    blocks = own_rows // CHUNK
-
     def mesh_copy(block, k):
         peer = rank_peer(k)
         at = pl.ds(pl.multiple_of(rank * own_rows + block * CHUNK, CHUNK), CHUNK)
@@ -463,18 +484,28 @@
             finished_mesh.at[rank, pl.ds(pl.multiple_of(block * CHUNK, CHUNK), CHUNK)], mesh_out.at[at], mesh_own.at[block]
         )
 
+    @pl.loop(0, far_count + near_count)
+    def _(j):
+        paired = 2 * min(far_count, near_count)
+        odd = lax.rem(j, 2)
+        rest = (far_first if far_count > near_count else OWN_CHUNKS) + j - paired // 2
+        chunk = jnp.where(j < paired, jnp.where(odd == 0, far_first, OWN_CHUNKS) + j // 2, rest)
+
+        @pl.when(chunk >= far_first)
+        def _():
+            await_message(chunk, FAR_ROWS)
+
+        @pl.when(chunk < far_first)
+        def _():
+            await_message(chunk, NEAR_ROWS)
+
+        add_messages(chunk)
+
     @pl.loop(0, blocks)
     def _(block):
         at = pl.ds(pl.multiple_of(block * CHUNK, CHUNK), CHUNK)
-        line = iota((CHUNK, CHUNK), 0) + block * CHUNK
-        total = None
-        for chunk, (k, c) in enumerate(plan):
-            row = k * CLASS_ROWS + 2 * c
-            wanted = jnp.concatenate([reqs[row : row + 1, :], reqs[row + 1 : row + 2, :]], axis=1)
-            piece = dot(one_hot(line == wanted), messages[chunk])
-            total = piece if total is None else total + piece
         own = mesh_v[at, :]
-        pre = dot(own, third_w[:full, :]) + dot(total.astype(jnp.bfloat16), third_w[full:, :]) + vector_row(4)
+        pre = dot(own, third_w[:full, :]) + dot(summed[at, :].astype(jnp.bfloat16), third_w[full:, :]) + vector_row(4)
         hidden = jax.nn.silu(pre).astype(jnp.bfloat16)
         total = dot(hidden, fourth_w[...]) + vector_row(5)
         update = normalize(total, vector_row(6), vector_row(7))
@@ -571,10 +602,11 @@
             pltpu.VMEM((ranks, chunks, CHUNK, width), bf16),
             pltpu.VMEM((ranks, chunks, CHUNK, width), bf16),
             pltpu.VMEM((ranks * max(edge_rows, chunks * CHUNK), width), f32),
-            pltpu.VMEM((CHUNK, full), f32),
+            pltpu.VMEM((ranks, CHUNK, width), f32),
             pltpu.VMEM((128, width), f32),
             pltpu.VMEM((edge_rows, width), bf16),
             pltpu.VMEM((ranks, own_rows, width), bf16),
+            pltpu.VMEM((own_rows, full), f32),
             dma((12,)),
             dma((3, 8)),
             dma((3, 8)),

time: 147 us -> 132 us (0.90)
  Pallas kernels: 139 us -> 125 us
    pallas_call x1, Pallas kernels: 139 us -> 125 us  [run_stages(): pl.pallas_call(functools.partial(stage_kernel, (patches, ranks, mesh_rows...]
where the time goes in v3:
time: 132 us
  Pallas kernels  125 us (95%)
  local copies, waits for them, and re-layouts  5.13 us (4%)
  between operations  1.95 us (1%)
    pallas_call x1, Pallas kernels, run_stages(): pl.pallas_call(functools.partial(stage_kernel, (patches, ranks, mesh_rows...  125 us
    unnamed x4, local copies, waits for them, and re-layouts  3.93 us

profile of v3, /device:TPU:1, one launch (start us, length us, event | category | flops | bytes accessed | tf_op | source)
XLA Modules:
  0.0 131.8 jit_solution(9312610464912882354)
XLA Ops:
  1.3 124.5 %run_stages.1 = (bf16[5120,128]{1,0:T(8,128)(2,1)}, bf16[8192,128]{1,0:T(8,128)(2,1)}, s32[8,128]{1,0:T(8,128)}) custom-call(s32[1]{0:T(128)S(6)} %copy.69.count, s32[64,128]{1,0:T(8,128)} %bitcast.42, s32[64,128]{1,0:T(8,128)} %bitcast.43, s32[320,128]{1,0:T(8,128)} %bitcast.41, f32[1,128]{1,0:T(1,128)} %bitcast.57, f32[1,128]{1,0:T(1,128)} %bitcast.51, ...), custom_call_target="tpu_custom_call" | custom-call | tf_op jit(solution)/shard_map/run_stages/pallas_call | solution.py:567
  125.8 1.2 slice.34
  127.6 0.2 conditional.1
  127.9 0.0 copy-start.2
  127.9 2.6 %copy.70 = bf16[5120,128]{1,0:T(8,128)(2,1)} copy(bf16[5120,128]{1,0:T(8,128)(2,1)} %get-tuple-element.852) | data formatting | bytes 2621440
  130.5 0.0 copy-done.2
  130.5 1.3 %copy.71 = bf16[8192,128]{1,0:T(8,128)(2,1)} copy(bf16[8192,128]{1,0:T(8,128)(2,1)S(1)} %copy-done.2) | data formatting | bytes 4194304
Async XLA Ops:
  127.9 2.6 %copy-start.2 = (bf16[8192,128]{1,0:T(8,128)(2,1)S(1)}, bf16[8192,128]{1,0:T(8,128)(2,1)}, u32[]{:S(2)}) copy-start(bf16[8192,128]{1,0:T(8,128)(2,1)} %get-tuple-element.853) | copy-start | bytes 6291460

commit v4 on v3

--- a/solution.py
+++ b/solution.py
@@ -13,6 +13,7 @@
 NEAR_CHUNKS = 2
 NEAR_ROWS = 240
 FAR_ROWS = 176
+FAR_FIRST = 128
 CLASS_ROWS = 8
 
 
@@ -56,6 +57,10 @@
     near = NEAR_CHUNKS * NEAR_ROWS
     caps = [OWN_CHUNKS * CHUNK, near] + [FAR_ROWS] * (patches - 3) + [near]
     return starts, caps, OWN_CHUNKS + 2 * NEAR_CHUNKS + patches - 3
+
+
+def early_blocks(own_rows):
+    return (own_rows // CHUNK * 3) // 5
 
 
 def plan_edges(sizes, me, rank_me, count, recv_ref, send_ref, slot_ref, req_ref, edge_ref, send_out_ref, where_ref, slots, target, masks, position, local, totals):
@@ -97,18 +102,32 @@
     classes = patches * ranks
     for c in range(classes):
         masks[c * groups : (c + 1) * groups, :] = one_hot(label == c)
+    early = inside - part * own_rows < early_blocks(own_rows) * CHUNK
+    far = range(2 * ranks, (patches - 1) * ranks)
+    for c in far:
+        at = (classes + c - far[0]) * groups
+        masks[at : at + groups, :] = one_hot((label == c) & early)
     steps = jnp.concatenate([one_hot(iota((128, 128), 0) <= iota((128, 128), 1)), jnp.ones((128, 128), jnp.bfloat16)], axis=1)
-    totals[...] = dot(masks[...], steps)
+    size = masks.shape[0]
+    for half in range(2):
+        totals[half * size : (half + 1) * size, :] = dot(masks[...], steps[:, half * 128 : (half + 1) * 128])
     below = one_hot(iota((groups, groups), 1) < iota((groups, groups), 0))
     rank = jnp.zeros(shape, jnp.float32)
     over = jnp.zeros((1, 128), jnp.float32)
     for c in range(classes):
-        block = totals[c * groups : (c + 1) * groups, :]
-        inner, whole = block[:, :128], block[:, 128:]
+        inner = totals[c * groups : (c + 1) * groups, :]
+        whole = totals[size + c * groups : size + (c + 1) * groups, :]
         before = dot(below, whole.astype(jnp.bfloat16))
         mine = jnp.where(label == c, 1.0, 0.0)
-        rank = rank + mine * (inner - 1.0 + before)
         full = before[groups - 1 :, :] + whole[groups - 1 :, :]
+        spots = inner - 1.0 + before
+        if c in far:
+            at = (classes + c - far[0]) * groups
+            ahead = totals[at : at + groups, :] + dot(below, totals[size + at : size + at + groups, :].astype(jnp.bfloat16))
+            count_ahead = ahead[groups - 1 :, 127:]
+            spots = jnp.where(early, ahead - 1.0, spots + count_ahead - ahead)
+            over = jnp.maximum(over, jnp.where(count_ahead > float(FAR_FIRST), 1.0, 0.0))
+        rank = rank + mine * spots
         over = jnp.maximum(over, jnp.where(full > float(caps[c // ranks]), 1.0, 0.0))
     rank = rank.astype(jnp.int32)
     first = jnp.zeros(shape, jnp.int32)
@@ -158,7 +177,7 @@
     return finish
 
 
-def stage_kernel(sizes, count, receivers, senders, mesh_slot, bias_a, bias_b, gain_a, shift_a, bias_c, bias_d, gain_b, shift_b, w_edge, w_sender, w_receiver, w_edge_out, w_mesh_in, w_message_in, w_mesh_out, mesh, edge, grid, mesh_out, edge_out, flag, mesh_v, edge_v, grid_v, first_w, second_w, third_w, fourth_w, vectors, req, reqs, edges, sends, places, slots, target, masks, position, local, totals, edge_s, where, rows_out, rows_in, results, messages, outgoing, incoming, table, gathered, staged, finished, finished_mesh, summed, local_sem, weight_send, weight_recv, req_send, req_recv, row_send, row_recv, msg_send, msg_recv, out_send, out_recv, mesh_send, mesh_recv, mesh_own):
+def stage_kernel(sizes, count, receivers, senders, mesh_slot, bias_a, bias_b, gain_a, shift_a, bias_c, bias_d, gain_b, shift_b, w_edge, w_sender, w_receiver, w_edge_out, w_mesh_in, w_message_in, w_mesh_out, mesh, edge, grid, mesh_out, edge_out, flag, mesh_v, edge_v, grid_v, first_w, second_w, third_w, fourth_w, vectors, req, reqs, edges, sends, places, slots, target, masks, position, local, edge_s, where, rows_out, rows_in, results, messages, outgoing, incoming, table, gathered, staged, finished, finished_mesh, summed, local_sem, weight_send, weight_recv, req_send, req_recv, row_send, row_recv, msg_send, msg_recv, out_send, out_recv, mesh_send, mesh_recv, mesh_own):
     patches, ranks = sizes[0], sizes[1]
     me, rank = lax.axis_index("patch"), lax.axis_index("hidden")
     chunks = class_plan(patches)[2]
@@ -240,7 +259,7 @@
         weight_copy(n, 1).start()
         weight_copy(n, 0).start()
 
-    finish_plan = plan_edges(sizes, me, rank, count[0], receivers, senders, mesh_slot, req, edges, sends, places, slots, target, masks, position, local, totals)
+    finish_plan = plan_edges(sizes, me, rank, count[0], receivers, senders, mesh_slot, req, edges, sends, places, slots, target, masks, position, local, table)
 
     req_copies = []
     for k in range(1, patches):
@@ -285,10 +304,11 @@
             rows_out.at[chunk, part], rows_in.at[chunk, part], row_send.at[chunk], row_recv.at[chunk], "patch", patch_peer(-k)
         )
 
-    def msg_copy(chunk, k, rows):
-        part = pl.ds(0, rows)
+    def msg_copy(chunk, k, rows, late=False):
+        part = pl.ds(FAR_FIRST, rows - FAR_FIRST) if late else pl.ds(0, FAR_FIRST if rows == FAR_ROWS else rows)
+        n = 1 if late else 0
         return send(
-            results.at[chunk, part], messages.at[chunk, part], msg_send.at[chunk], msg_recv.at[chunk], "patch", patch_peer(k)
+            results.at[chunk, part], messages.at[chunk, part], msg_send.at[n, chunk], msg_recv.at[n, chunk], "patch", patch_peer(k)
         )
 
     def out_copy(chunk, k, rows):
@@ -351,13 +371,9 @@
 
     def edge_stage(chunk, rows):
         k, at = class_of(chunk)
-        if rows == CHUNK:
-            @pl.loop(0, 2)
-            def _(half):
-                collect(k * CLASS_ROWS + 2 * at + half, pl.multiple_of(half * 128, 128), 128)
-        else:
-            collect(k * CLASS_ROWS + 2 * at, 0, 128)
-            collect(k * CLASS_ROWS + 2 * at + 1, 128, rows - 128)
+        @pl.loop(0, 2)
+        def _(half):
+            collect(k * CLASS_ROWS + 2 * at + half, pl.multiple_of(half * 128, 128), 128)
         own_edge = jnp.concatenate([gathered[j, :rows, :] for j in range(ranks)], axis=1)
         pre = dot(own_edge.astype(jnp.bfloat16), first_w[:full, :])
         sender = pick(columns(sends, k, at)[:rows], grid_v, 1024)
@@ -392,6 +408,10 @@
 
     in_turn(remote_chunk)
 
+    @pl.loop(far_first, chunks)
+    def _(chunk):
+        msg_copy(chunk, class_of(chunk)[0], FAR_ROWS, True).start()
+
     for n in mesh_weights:
         weight_copy(n, 1).wait_recv()
         weight_copy(n, 2).start()
@@ -418,53 +438,23 @@
     def await_message(chunk, rows):
         msg_copy(chunk, class_of(chunk)[0], rows).wait_recv()
 
-    def add_messages(chunk):
+    def add_messages(chunk, first=0, last=blocks, depth=CHUNK):
         k, at = class_of(chunk)
         row = pl.multiple_of(k * CLASS_ROWS, CLASS_ROWS)
         asked = reqs[pl.ds(row, CLASS_ROWS), :]
         line = iota(asked.shape, 0)
         pair = [jnp.sum(jnp.where(line == 2 * at + n, asked, 0), axis=0, keepdims=True) for n in range(2)]
         wanted = jnp.concatenate(pair, axis=1)
-        for block in range(blocks):
+        for block in range(first, last):
             span = slice(block * CHUNK, (block + 1) * CHUNK)
-            hot = one_hot(iota((CHUNK, CHUNK), 0) + block * CHUNK == wanted)
-            summed[span, :] += dot(hot, messages[chunk])
+            hot = one_hot(iota((CHUNK, depth), 0) + block * CHUNK == wanted[:, :depth])
+            summed[span, :] += dot(hot, messages[chunk, :depth, :])
 
     summed[...] = jnp.zeros(summed.shape, jnp.float32)
 
     @pl.loop(0, OWN_CHUNKS)
     def _(chunk):
         add_messages(chunk)
-
-    each_chunk(await_out)
-
-    @pl.loop(0, ranks)
-    def _(j):
-        @pl.when(j == rank)
-        def _():
-            @pl.loop(0, chunks)
-            def _(chunk):
-                table[pl.ds(pl.multiple_of((j * chunks + chunk) * CHUNK, CHUNK), CHUNK), :] = outgoing[j, chunk].astype(jnp.float32)
-
-        @pl.when(j != rank)
-        def _():
-            @pl.loop(0, chunks)
-            def _(chunk):
-                table[pl.ds(pl.multiple_of((j * chunks + chunk) * CHUNK, CHUNK), CHUNK), :] = incoming[j, chunk].astype(jnp.float32)
-
-    own_columns = pl.ds(pl.multiple_of(rank * width, width), width)
-
-    @pl.loop(0, edge_rows // 128)
-    def _(line):
-        for n in range(128):
-            spot = within(where[line, n], table.shape[0])
-            staged[n : n + 1, :] = table[pl.ds(spot, 1), :]
-        at = pl.ds(pl.multiple_of(line * 128, 128), 128)
-        live = iota((128, width), 0) + line * 128 < count[0]
-        finished[at, :] = jnp.where(live, staged[...], edge_v[at, own_columns].astype(jnp.float32)).astype(jnp.bfloat16)
-
-    last = pltpu.make_async_copy(finished, edge_out, local_sem.at[0])
-    last.start()
 
     for n in mesh_weights:
         weight_copy(n, 0).wait_recv()
@@ -494,15 +484,22 @@
         @pl.when(chunk >= far_first)
         def _():
             await_message(chunk, FAR_ROWS)
+            add_messages(chunk, 0, early_blocks(own_rows), FAR_FIRST)
 
         @pl.when(chunk < far_first)
         def _():
             await_message(chunk, NEAR_ROWS)
-
-        add_messages(chunk)
+            add_messages(chunk)
 
     @pl.loop(0, blocks)
     def _(block):
+        @pl.when(block == early_blocks(own_rows))
+        def _():
+            @pl.loop(far_first, chunks)
+            def _(chunk):
+                msg_copy(chunk, class_of(chunk)[0], FAR_ROWS, True).wait_recv()
+                add_messages(chunk, early_blocks(own_rows), blocks)
+
         at = pl.ds(pl.multiple_of(block * CHUNK, CHUNK), CHUNK)
         own = mesh_v[at, :]
         pre = dot(own, third_w[:full, :]) + dot(summed[at, :].astype(jnp.bfloat16), third_w[full:, :]) + vector_row(4)
@@ -516,11 +513,41 @@
             mesh_copy(block, k).start()
         mesh_local(block).start()
 
+    each_chunk(await_out)
+
+    @pl.loop(0, ranks)
+    def _(j):
+        @pl.when(j == rank)
+        def _():
+            @pl.loop(0, chunks)
+            def _(chunk):
+                table[pl.ds(pl.multiple_of((j * chunks + chunk) * CHUNK, CHUNK), CHUNK), :] = outgoing[j, chunk].astype(jnp.float32)
+
+        @pl.when(j != rank)
+        def _():
+            @pl.loop(0, chunks)
+            def _(chunk):
+                table[pl.ds(pl.multiple_of((j * chunks + chunk) * CHUNK, CHUNK), CHUNK), :] = incoming[j, chunk].astype(jnp.float32)
+
+    own_columns = pl.ds(pl.multiple_of(rank * width, width), width)
+
+    @pl.loop(0, edge_rows // 128)
+    def _(line):
+        for n in range(128):
+            spot = within(where[line, n], table.shape[0])
+            staged[n : n + 1, :] = table[pl.ds(spot, 1), :]
+        at = pl.ds(pl.multiple_of(line * 128, 128), 128)
+        live = iota((128, width), 0) + line * 128 < count[0]
+        finished[at, :] = jnp.where(live, staged[...], edge_v[at, own_columns].astype(jnp.float32)).astype(jnp.bfloat16)
+
+    last = pltpu.make_async_copy(finished, edge_out, local_sem.at[0])
+    last.start()
+
     over = reqs[CLASS_ROWS - 1 : CLASS_ROWS, :]
     for k in range(1, patches):
         row = (k + 1) * CLASS_ROWS - 1
         over = jnp.maximum(over, reqs[row : row + 1, :])
-    flag[...] = jnp.broadcast_to(over, flag.shape)
+    flag[0] = jnp.max(over)
 
     for copy in req_copies:
         copy.wait_send()
@@ -535,6 +562,8 @@
             k = class_of(chunk)[0]
             row_copy(chunk, k, rows).wait_send()
             msg_copy(chunk, k, rows).wait_send()
+            if rows == FAR_ROWS:
+                msg_copy(chunk, k, rows, True).wait_send()
 
     each_chunk(drain)
 
@@ -563,15 +592,15 @@
     hbm = pl.BlockSpec(memory_space=pl.ANY)
     blocks = own_rows // CHUNK
     lists = patches * CLASS_ROWS
-    classes = patches * ranks * groups
+    classes = (patches + patches - 3) * ranks * groups
     return pl.pallas_call(
         functools.partial(stage_kernel, (patches, ranks, mesh_rows, grid_rows, parts)),
         in_specs=[smem] + [vmem] * 11 + [hbm] * 10,
-        out_specs=[hbm, hbm, vmem],
+        out_specs=[hbm, hbm, smem],
         out_shape=[
             jax.ShapeDtypeStruct((mesh_rows, width), bf16),
             jax.ShapeDtypeStruct((edge_rows, width), bf16),
-            jax.ShapeDtypeStruct((8, 128), i32),
+            jax.ShapeDtypeStruct((1,), i32),
         ],
         scratch_shapes=[
             pltpu.VMEM((own_rows, full), bf16),
@@ -592,7 +621,6 @@
             pltpu.VMEM((classes, 128), bf16),
             pltpu.VMEM((groups, 128), i32),
             pltpu.VMEM((groups, 128), i32),
-            pltpu.VMEM((classes, 256), f32),
             pltpu.SMEM((lists, 128), i32),
             pltpu.SMEM((groups, 128), i32),
             pltpu.VMEM((chunks, CHUNK, full), bf16),
@@ -614,8 +642,8 @@
             dma((patches,)),
             dma((chunks,)),
             dma((chunks,)),
-            dma((chunks,)),
-            dma((chunks,)),
+            dma((2, chunks)),
+            dma((2, chunks)),
             dma((ranks, chunks)),
             dma((ranks, chunks)),
             dma((ranks, blocks)),
@@ -701,8 +729,8 @@
         part = sums[k * mesh_rows : (k + 1) * mesh_rows].astype(bf16)
         part = lax.ppermute(part, "patch", [(j, (j + k) % patches) for j in range(patches)])
         summed = summed + part.astype(jnp.float32)
-    summed = jnp.roll(turn(summed.astype(bf16), 1), rank * width, 1)
-    pre = dot(mesh_latent, w_mesh_in) + dot(summed, w_message_in) + mesh_bias[None]
+    turned = jnp.roll(w_message_in, -rank * width, 0)
+    pre = dot(mesh_latent, w_mesh_in) + dot(turn(summed.astype(bf16), 1), turned) + mesh_bias[None]
     update = spread_mlp(pre, w_mesh_out, mesh_out_bias, mesh_gain, mesh_shift)
     mesh_out = (own(mesh_latent).astype(jnp.float32) + update).astype(bf16)
     return mesh_out, edge_out
@@ -730,7 +758,7 @@
         patches, ranks, edge_counts, receivers, senders, mesh_slot, vectors, weights, mesh_latent, edge_latent, grid_latent
     )
     return lax.cond(
-        flag[0, 0] > 0,
+        flag[0] > 0,
         lambda outs, args: dense(patches, ranks, args),
         lambda outs, args: outs,
         (mesh_out, edge_out),

time: 132 us -> 122 us (0.924); the launches traced: 132 us -> 120 us
  Pallas kernels: 125 us -> 114 us
    pallas_call x1, Pallas kernels: 125 us -> 114 us  [run_stages(): pl.pallas_call(functools.partial(stage_kernel, (patches, ranks, mesh_rows...]
where the time goes in v4:
time: 122 us; the launch traced here: 120 us
  Pallas kernels  114 us (93%)
  local copies, waits for them, and re-layouts  3.93 us (3%)
  between operations  1.87 us (2%)
    pallas_call x1, Pallas kernels, run_stages(): pl.pallas_call(functools.partial(stage_kernel, (patches, ranks, mesh_rows...  114 us
    unnamed x4, local copies, waits for them, and re-layouts  3.93 us

profile of v4, /device:TPU:1, one launch (start us, length us, event | category | flops | bytes accessed | tf_op | source)
XLA Modules:
  0.0 119.9 jit_solution(10477425594715212187)
XLA Ops:
  1.3 113.9 %run_stages.1 = (bf16[5120,128]{1,0:T(8,128)(2,1)}, bf16[8192,128]{1,0:T(8,128)(2,1)}, s32[1]{0:T(128)}) custom-call(s32[1]{0:T(128)S(6)} %copy.62.count, s32[64,128]{1,0:T(8,128)} %bitcast.41, s32[64,128]{1,0:T(8,128)} %bitcast.42, s32[320,128]{1,0:T(8,128)} %bitcast.40, f32[1,128]{1,0:T(1,128)} %bitcast.55, f32[1,128]{1,0:T(1,128)} %bitcast.49, ...), custom_call_target="tpu_custom_call" | custom-call | tf_op jit(solution)/shard_map/run_stages/pallas_call | solution.py:596
  115.7 0.3 conditional.1
  116.0 0.0 copy-start.2
  116.0 2.6 %copy.63 = bf16[5120,128]{1,0:T(8,128)(2,1)} copy(bf16[5120,128]{1,0:T(8,128)(2,1)} %get-tuple-element.850) | data formatting | bytes 2621440
  118.6 0.0 copy-done.2
  118.6 1.3 %copy.64 = bf16[8192,128]{1,0:T(8,128)(2,1)} copy(bf16[8192,128]{1,0:T(8,128)(2,1)S(1)} %copy-done.2) | data formatting | bytes 4194304
Async XLA Ops:
  116.0 2.6 %copy-start.2 = (bf16[8192,128]{1,0:T(8,128)(2,1)S(1)}, bf16[8192,128]{1,0:T(8,128)(2,1)}, u32[]{:S(2)}) copy-start(bf16[8192,128]{1,0:T(8,128)(2,1)} %get-tuple-element.851) | copy-start | bytes 6291460
